TPU v7x, 32 devices: a whole 2x2x4 slice. The times are simulated.
32 devices in a mesh: sample: 2 (over x), fsdp: 4 (over z), seq: 4 (over y, core).
Axes of the slice: x: 2, y: 2, z: 4, core: 2. Of those that a mesh axis runs over, the one named last changes fastest.
Arguments:
- token_act: bfloat16 [8, 512, 768], P(('sample', 'fsdp'), 'seq'), may hold values from -40 to 40
- token_cond: bfloat16 [8, 512, 768], P(('sample', 'fsdp'), 'seq'), may hold values from -40 to 40
- pair_bias: bfloat16 [16, 512, 512], P('fsdp', 'seq'), may hold values from -8 to 296
- token_mask: int32 [512], P('seq'), may hold values 0 or 1
- ada_weights: bfloat16 [4, 768, 768], P(None, None, 'fsdp'), may hold values from -0.21875 to 0.21875
- attention_in: bfloat16 [4, 768, 768], P(None, None, 'fsdp'), may hold values from -0.21875 to 0.21875
- attention_out: bfloat16 [768, 768], P('fsdp'), may hold values from -0.21875 to 0.21875
- transition_in: bfloat16 [2, 768, 1536], P(None, None, 'fsdp'), may hold values from -0.21875 to 0.21875
- transition_out: bfloat16 [1536, 768], P('fsdp'), may hold values from -0.15625 to 0.15625
- token_vectors: float32 [3, 768], replicated, may hold values from -4 to 4
- atom_skip: bfloat16 [8, 4096, 128], P(('sample', 'fsdp'), 'seq'), may hold values from -40 to 40
- atom_cond: bfloat16 [4096, 128], P('seq'), may hold values from -40 to 40
- atom_bias: bfloat16 [4, 4096, 128], P(None, 'seq'), may hold values from -6 to 296
- window_bounds: int32 [128, 2], P('seq'), may hold values from 0 to 4096, as said below
- atom_token: int32 [4096], P('seq'), may hold values from 0 to 511, as said below
- atom_weights: bfloat16 [7, 128, 128], P(None, None, 'fsdp'), may hold values from -0.5 to 0.5
- token_to_atom: bfloat16 [768, 128], P('fsdp'), may hold values from -0.21875 to 0.21875
- atom_vectors: float32 [2, 128], replicated, may hold values from -4 to 4
- position_out: bfloat16 [3, 128], replicated, may hold values from -0.5 to 0.5
Outputs:
- token_out: bfloat16 [8, 512, 768], P(('sample', 'fsdp'), 'seq')
- position_update: float32 [8, 3, 4096], P(('sample', 'fsdp'), None, 'seq')
Inputs may be any that keep to these rules, and one draw needn't show every extreme that they name: `window_bounds`: row b belongs to the atoms 32 * b to 32 * b + 31; column 0 is at least 0 and at least 32 * b - 48, and at most 32 * b; column 1 is at least 32 * b + 32, at most 32 * b + 80 and at most 4096. `atom_token`: atoms are numbered in token order: the value never falls from one atom to the next, the first atom belongs to token 0, the last to token 511, and every token owns 1 to 24 atoms.
All inputs are finite; a program needn't handle non-finite values. No bound on the sum of `token_mask` on one device may be relied on, other than what follows from the above.
Results may differ from a plain program's by a relative error of at most 0.014.
Values may be sent and summed in bfloat16 or wider, within the bound.
A program may use at most 128 MiB of HBM per device.

v0:
```python
import functools
import math

import jax
import jax.numpy as jnp
from jax import lax
from jax.experimental import pallas as pl
from jax.experimental.pallas import tpu as pltpu
from jax.sharding import PartitionSpec as P

HA = 4
WQ = 32
WK = 128
HD = 48
EPS = 1e-05
FAR = -1e30
RIM = (WK - WQ) // 2
VMEM_LIMIT = 56 * 1024 * 1024
MESH = pl.DeviceIdType.MESH


def layer_norm(values):
    values = values.astype(jnp.float32)
    center = values - jnp.mean(values, axis=-1, keepdims=True)
    spread = jnp.mean(center * center, axis=-1, keepdims=True)
    return center * lax.rsqrt(spread + EPS)


def matmul(left_side, right_side):
    return jnp.dot(left_side, right_side, preferred_element_type=jnp.float32)


def pack(array):
    half = array.shape[-2] // 2
    return jnp.concatenate([array[..., :half, :], array[..., half:, :]], axis=-1)


def unpack(array):
    half = array.shape[-1] // 2
    return jnp.concatenate([array[..., :half], array[..., half:]], axis=-2)


class Line:
    def __init__(self, axis, size, paired, block, out, send, recv, local, partner_send, partner_recv):
        self.axis, self.size, self.paired = axis, size, paired
        self.block, self.out, self.send, self.recv, self.local = block, out, send, recv, local
        self.partner_send, self.partner_recv = partner_send, partner_recv
        self.index = lax.axis_index(axis)
        self.stride = 2 if paired else 1
        self.length = size // self.stride
        self.position = self.index // 2 if paired else self.index
        self.parity = self.index - 2 * self.position if paired else 0

    def slot(self, position):
        return position * self.stride + self.parity

    def partner(self):
        return self.index + 1 - 2 * self.parity

    def guards(self, side, step):
        here, last = self.position, self.length - 1
        if side == 0:
            return (here - step >= 0) & (here < last), here - 1 - step >= 0
        return (here + step <= last) & (here > 0), here + 1 + step <= last

    def copy(self, side, step, arriving):
        sign = 1 if side == 0 else -1
        origin = self.position - sign * (step + (1 if arriving else 0))
        target = self.slot(self.position + sign)
        slot = self.slot(origin)
        source = self.block if (step == 0 and not arriving) else self.out.at[slot]
        return pltpu.make_async_remote_copy(
            src_ref=source,
            dst_ref=self.out.at[slot],
            send_sem=self.send.at[side, step],
            recv_sem=self.recv.at[side, step],
            device_id={self.axis: target},
            device_id_type=MESH,
        )

    def hand(self, key, origin, own, arriving):
        slot = self.slot(origin)
        landing = origin * 2 + 1 - self.parity if arriving else slot
        return pltpu.make_async_remote_copy(
            src_ref=self.block if own else self.out.at[slot],
            dst_ref=self.out.at[landing],
            send_sem=self.partner_send.at[key],
            recv_sem=self.partner_recv.at[key],
            device_id={self.axis: self.partner()},
            device_id_type=MESH,
        )

    def greet(self, barrier):
        def neighbour(target):
            pl.semaphore_signal(barrier, inc=1, device_id={self.axis: target}, device_id_type=MESH)

        expected = 0
        if self.length > 1:
            above = self.position > 0
            below = self.position < self.length - 1

            @pl.when(above)
            def _():
                neighbour(self.slot(self.position - 1))

            @pl.when(below)
            def _():
                neighbour(self.slot(self.position + 1))

            expected = jnp.where(above, 1, 0) + jnp.where(below, 1, 0)
        if self.paired:
            neighbour(self.partner())
            expected = expected + 1
        return expected

    def begin(self):
        pltpu.make_async_copy(self.block, self.out.at[self.index], self.local.at[0]).start()
        if self.paired:
            self.hand(0, self.position, True, False).start()

    def advance(self, step):
        for side in (0, 1):
            goes, unused = self.guards(side, step)
            if step > 0:
                self.arrive(side, step - 1)

            @pl.when(goes)
            def _():
                self.copy(side, step, False).start()

    def arrive(self, side, step):
        unused, comes = self.guards(side, step)

        @pl.when(comes)
        def _():
            self.copy(side, step, True).wait_recv()
            if self.paired:
                origin = self.position - (step + 1) if side == 0 else self.position + step + 1
                self.hand(1 + side * (self.length - 1) + step, origin, False, False).start()

    def steps(self):
        return self.length - 1

    def finish(self):
        last = self.length - 1
        if last > 0:
            for side in (0, 1):
                self.arrive(side, last - 1)
        for side in (0, 1):
            for step in range(last):
                goes, comes = self.guards(side, step)

                @pl.when(goes)
                def _():
                    self.copy(side, step, False).wait_send()

                if self.paired:

                    @pl.when(comes)
                    def _():
                        origin = self.position - (step + 1) if side == 0 else self.position + step + 1
                        key = 1 + side * last + step
                        self.hand(key, origin, False, False).wait_send()
                        self.hand(key, origin, False, True).wait_recv()

        if self.paired:
            self.hand(0, self.position, True, False).wait_send()
            self.hand(0, self.position, True, True).wait_recv()
        pltpu.make_async_copy(self.block, self.out.at[self.index], self.local.at[0]).wait()


class Exchange:
    def __init__(self, axis, size, block, out, send, recv, local):
        self.axis, self.size, self.block, self.out = axis, size, block, out
        self.send, self.recv, self.local = send, recv, local
        self.index = lax.axis_index(axis)

    def peer(self, shift):
        return lax.rem(self.index + shift, self.size)

    def greet(self, barrier):
        for shift in range(1, self.size):
            pl.semaphore_signal(
                barrier, inc=1, device_id={self.axis: self.peer(shift)}, device_id_type=MESH
            )
        return self.size - 1

    def copy(self, shift, arriving):
        landing = self.peer(self.size - shift) if arriving else self.index
        return pltpu.make_async_remote_copy(
            src_ref=self.block.at[self.peer(shift)],
            dst_ref=self.out.at[landing],
            send_sem=self.send.at[shift],
            recv_sem=self.recv.at[shift],
            device_id={self.axis: self.peer(shift)},
            device_id_type=MESH,
        )

    def begin(self):
        pltpu.make_async_copy(
            self.block.at[self.index], self.out.at[self.index], self.local.at[0]
        ).start()
        for shift in range(1, self.size):
            self.copy(shift, False).start()

    def steps(self):
        return 0

    def advance(self, step):
        pass

    def finish(self):
        for shift in range(1, self.size):
            self.copy(shift, False).wait_send()
            self.copy(shift, True).wait_recv()
        pltpu.make_async_copy(
            self.block.at[self.index], self.out.at[self.index], self.local.at[0]
        ).wait()


class Halo:
    def __init__(self, axis, size, block, out, send, recv):
        self.axis, self.size, self.block, self.out = axis, size, block, out
        self.send, self.recv = send, recv
        self.index = lax.axis_index(axis)
        self.above, self.below = self.index > 0, self.index < size - 1

    def greet(self, barrier):
        for present, target in ((self.above, self.index - 1), (self.below, self.index + 1)):

            @pl.when(present)
            def _():
                pl.semaphore_signal(
                    barrier, inc=1, device_id={self.axis: target}, device_id_type=MESH
                )

        return jnp.where(self.above, 1, 0) + jnp.where(self.below, 1, 0)

    def copy(self, side):
        return pltpu.make_async_remote_copy(
            src_ref=self.block.at[side],
            dst_ref=self.out.at[1 - side],
            send_sem=self.send.at[side],
            recv_sem=self.recv.at[side],
            device_id={self.axis: self.index - 1 + 2 * side},
            device_id_type=MESH,
        )

    def begin(self):
        for side, present in ((0, self.above), (1, self.below)):

            @pl.when(present)
            def _():
                self.copy(side).start()

            @pl.when(jnp.logical_not(present))
            def _():
                self.out[side] = jnp.zeros(self.out.shape[1:], self.out.dtype)

    def steps(self):
        return 0

    def finish(self):
        for side, present in ((0, self.above), (1, self.below)):

            @pl.when(present)
            def _():
                self.copy(side).wait_send()
                self.copy(1 - side).wait_recv()


class Swap:
    def __init__(self, axis, size, block, out, send, recv, local):
        self.axis, self.block, self.out = axis, block, out
        self.send, self.recv, self.local = send, recv, local
        self.index = lax.axis_index(axis)
        self.parity = lax.rem(self.index, 2)

    def copy(self, arriving):
        return pltpu.make_async_remote_copy(
            src_ref=self.block,
            dst_ref=self.out.at[1 - self.parity if arriving else self.parity],
            send_sem=self.send.at[0],
            recv_sem=self.recv.at[0],
            device_id={self.axis: self.index + 1 - 2 * self.parity},
            device_id_type=MESH,
        )

    def begin(self):
        pltpu.make_async_copy(self.block, self.out.at[self.parity], self.local.at[0]).start()
        self.copy(False).start()

    def steps(self):
        return 0

    def finish(self):
        self.copy(False).wait_send()
        self.copy(True).wait_recv()
        pltpu.make_async_copy(self.block, self.out.at[self.parity], self.local.at[0]).wait()


def line_scratch(size, paired):
    dma = pltpu.SemaphoreType.DMA
    length = size // 2 if paired else size
    steps = max(length - 1, 1)
    scratch = [dma((2, steps)), dma((2, steps)), dma((1,))]
    if paired:
        scratch += [dma((2 * length,)), dma((2 * length,))]
    return scratch


def run_flows(flows):
    for flow in flows:
        flow.begin()
    for step in range(max(flow.steps() for flow in flows)):
        for flow in flows:
            if step < flow.steps():
                flow.advance(step)
    for flow in flows:
        flow.finish()


def move_kernel(kinds, *refs):
    count = len(kinds)
    blocks, outs, sems = refs[:count], refs[count : 2 * count], list(refs[2 * count :])
    flows, leaders = [], {}

    def take(number):
        taken = sems[:number]
        del sems[:number]
        return taken

    for (kind, axis, size, chunks), block, out in zip(kinds, blocks, outs):
        if kind == "exchange":
            flow = Exchange(axis, size, block, out, *take(3))
            leaders[axis] = flow
            flows.append(flow)
        elif kind == "halo":
            flows.append(Halo(axis, size, block, out, *take(2)))
        elif kind == "swap":
            flows.append(Swap(axis, size, block, out, *take(3)))
        else:
            paired = kind == "paired"
            rows = block.shape[0] // chunks
            for chunk in range(chunks):
                part = pl.ds(chunk * rows, rows)
                flow = Line(
                    axis, size, paired, block.at[part], ChunkedOut(out, part),
                    *take(5 if paired else 3), *(() if paired else (None, None)),
                )
                flows.append(flow)
        leaders.setdefault(axis, flows[-1])
    barrier = pltpu.get_barrier_semaphore()
    expected = 0
    for flow in leaders.values():
        expected = expected + flow.greet(barrier)
    pl.semaphore_wait(barrier, expected)
    run_flows(flows)


class ChunkedOut:
    def __init__(self, out, part):
        self.out, self.part = out, part

    @property
    def at(self):
        return self

    def __getitem__(self, slot):
        return self.out.at[slot, self.part]


def move(identity, items):
    kinds, arrays, shapes, scratch = [], [], [], []
    sent = 0
    for kind, axis, array, chunks in items:
        size = lax.axis_size(axis)
        kinds.append((kind, axis, size, chunks))
        arrays.append(array)
        lead = {"exchange": (), "halo": (), "swap": (2,)}.get(kind, (size,))
        shapes.append(jax.ShapeDtypeStruct(lead + array.shape, array.dtype))
        sent += array.size * array.dtype.itemsize
        dma = pltpu.SemaphoreType.DMA
        if kind == "exchange":
            scratch += [dma((size,)), dma((size,)), dma((1,))]
        elif kind == "halo":
            scratch += [dma((2,)), dma((2,))]
        elif kind == "swap":
            scratch += [dma((1,)), dma((1,)), dma((1,))]
        else:
            scratch += line_scratch(size, kind == "paired") * chunks
    return pl.pallas_call(
        functools.partial(move_kernel, tuple(kinds)),
        out_shape=tuple(shapes),
        in_specs=[pl.BlockSpec(memory_space=pltpu.VMEM)] * len(arrays),
        out_specs=tuple([pl.BlockSpec(memory_space=pltpu.VMEM)] * len(arrays)),
        scratch_shapes=scratch,
        compiler_params=pltpu.CompilerParams(
            collective_id=identity, has_side_effects=True, vmem_limit_bytes=VMEM_LIMIT
        ),
        cost_estimate=pl.CostEstimate(flops=0, bytes_accessed=30 * sent, transcendentals=0),
        name=f"move{identity}",
    )(*arrays)


def close_kernel(
    axis, size, row_axis, row_size, part_ref, act_ref, project_ref, token_ref, rows_ref,
    came_ref, block_ref, send, recv, local, *line_sems,
):
    line = Line(row_axis, row_size, True, block_ref, rows_ref, *line_sems)
    swap = Exchange(axis, size, part_ref, came_ref, send, recv, local)
    barrier = pltpu.get_barrier_semaphore()
    expected = line.greet(barrier) + swap.greet(barrier)
    pl.semaphore_wait(barrier, expected)
    swap.begin()
    swap.finish()
    total = act_ref[...].astype(jnp.float32)
    for origin in range(size):
        total = total + came_ref[origin].astype(jnp.float32)
    token = total.astype(jnp.bfloat16)
    token_ref[...] = token
    block_ref[...] = matmul(token, project_ref[...]).astype(jnp.bfloat16)
    run_flows([line])


def close(identity, axis, row_axis, parts, act_rows, project):
    size, row_size = lax.axis_size(axis), lax.axis_size(row_axis)
    rows, depth = act_rows.shape
    dma = pltpu.SemaphoreType.DMA
    vmem = pl.BlockSpec(memory_space=pltpu.VMEM)
    return pl.pallas_call(
        functools.partial(close_kernel, axis, size, row_axis, row_size),
        out_shape=(
            jax.ShapeDtypeStruct((rows, depth), jnp.bfloat16),
            jax.ShapeDtypeStruct((row_size, rows, project.shape[1]), jnp.bfloat16),
        ),
        in_specs=[vmem] * 3,
        out_specs=(vmem, vmem),
        scratch_shapes=[
            pltpu.VMEM(parts.shape, jnp.bfloat16),
            pltpu.VMEM((rows, project.shape[1]), jnp.bfloat16),
            dma((size,)),
            dma((size,)),
            dma((1,)),
        ]
        + line_scratch(row_size, True),
        compiler_params=pltpu.CompilerParams(
            collective_id=identity, has_side_effects=True, vmem_limit_bytes=VMEM_LIMIT
        ),
        name="close",
    )(parts, act_rows, project)


def attention_kernel(heads, span, q_ref, gate_ref, kv_ref, bias_ref, mask_ref, out_ref):
    rows, width = q_ref.shape[1], q_ref.shape[2]
    pieces, piece_rows = kv_ref.shape[0], kv_ref.shape[2]
    queries = q_ref[0]
    head_of = lax.broadcasted_iota(jnp.int32, (rows, width), 1) // HD
    stacked = jnp.concatenate(
        [jnp.where(head_of == head, queries, 0).astype(jnp.bfloat16) for head in range(heads)], axis=0
    )
    scale = 1.0 / math.sqrt(HD)
    maxima = totals = summed = None
    for first in range(0, pieces, span):
        taken = min(span, pieces - first)
        keys = jnp.concatenate([kv_ref[first + i, 0, :, :width] for i in range(taken)], axis=0)
        values = jnp.concatenate([kv_ref[first + i, 0, :, width:] for i in range(taken)], axis=0)
        columns = pl.ds(first * piece_rows, taken * piece_rows)
        scores = (
            lax.dot_general(
                stacked, keys, (((1,), (1,)), ((), ())), preferred_element_type=jnp.float32
            )
            * scale
        )
        bias = bias_ref[:, :, columns].reshape(heads * rows, taken * piece_rows)
        scores = scores + bias.astype(jnp.float32)
        scores = jnp.where(mask_ref[:, columns] > 0, scores, FAR)
        block_max = jnp.max(scores, axis=-1, keepdims=True)
        new_maxima = block_max if maxima is None else jnp.maximum(maxima, block_max)
        weights = jnp.exp(scores - new_maxima)
        block_total = jnp.sum(weights, axis=-1, keepdims=True)
        update = matmul(weights.astype(jnp.bfloat16), values)
        if maxima is None:
            totals, summed = block_total, update
        else:
            factor = jnp.exp(maxima - new_maxima)
            totals = totals * factor + block_total
            summed = summed * factor + update
        maxima = new_maxima
    attended = summed / totals
    result = jnp.zeros((rows, width), jnp.float32)
    for head in range(heads):
        result = result + jnp.where(head_of == head, attended[head * rows : (head + 1) * rows], 0.0)
    gate = jax.nn.sigmoid(gate_ref[0].astype(jnp.float32))
    out_ref[0] = (result * gate).astype(jnp.bfloat16)


def token_attention(query_rows, gate_rows, kv_all, pair_bias, mask_row):
    groups, rows, width = query_rows.shape
    heads, keys = pair_bias.shape[0], pair_bias.shape[2]
    pieces, piece_rows = kv_all.shape[0], kv_all.shape[2]
    one = lambda g: (g, 0, 0)
    return pl.pallas_call(
        functools.partial(attention_kernel, heads, max(512 // piece_rows, 1)),
        grid=(groups,),
        in_specs=[
            pl.BlockSpec((1, rows, width), one),
            pl.BlockSpec((1, rows, width), one),
            pl.BlockSpec((pieces, 1, piece_rows, 2 * width), lambda g: (0, g, 0, 0)),
            pl.BlockSpec((heads, rows, keys), lambda g: (0, 0, 0)),
            pl.BlockSpec((1, keys), lambda g: (0, 0)),
        ],
        out_specs=pl.BlockSpec((1, rows, width), one),
        out_shape=jax.ShapeDtypeStruct((groups, rows, width), jnp.bfloat16),
        compiler_params=pltpu.CompilerParams(vmem_limit_bytes=VMEM_LIMIT),
        name="token_attention",
    )(query_rows, gate_rows, kv_all, pair_bias, mask_row)


def atom_kernel(
    first_ref, bounds_ref, rows_ref, skip_ref, cond_ref, rim_ref, token_ref, weight_ref, vector_ref,
    position_ref, bias_ref, out_ref, state_ref, query_ref, gate_ref, key_ref, value_ref, held_ref,
):
    count, channels = query_ref.shape
    head_width = channels // HA
    tokens = rows_ref.shape[0]
    chunk = min(512, tokens)
    inner = pl.ds(RIM, count)
    owners = token_ref[...]
    taken = jnp.zeros((owners.shape[0], channels), jnp.float32)
    for start in range(0, tokens, chunk):
        column = lax.broadcasted_iota(jnp.int32, (owners.shape[0], chunk), 1) + start
        hit = jnp.where(owners == column, 1.0, 0.0).astype(jnp.bfloat16)
        taken = taken + matmul(hit, rows_ref[start : start + chunk, :])
    skip = jnp.concatenate([rim_ref[0, :, :channels], skip_ref[...], rim_ref[1, :, :channels]], axis=0)
    cond = jnp.concatenate([rim_ref[0, :, channels:], cond_ref[...], rim_ref[1, :, channels:]], axis=0)
    state = skip.astype(jnp.float32) + taken
    state_ref[...] = state
    normed = layer_norm(cond).astype(jnp.bfloat16)
    atom_x = (
        jax.nn.sigmoid(matmul(normed, weight_ref[0]) + vector_ref[0:1, :]) * layer_norm(state)
        + matmul(normed, weight_ref[1])
    ).astype(jnp.bfloat16)
    own_x = atom_x[RIM : RIM + count, :]
    query_ref[...] = (matmul(own_x, weight_ref[2]) + vector_ref[1:2, :]).astype(jnp.bfloat16)
    gate_ref[...] = matmul(own_x, weight_ref[5]).astype(jnp.bfloat16)
    key_ref[...] = matmul(atom_x, weight_ref[3]).astype(jnp.bfloat16)
    value_ref[...] = matmul(atom_x, weight_ref[4]).astype(jnp.bfloat16)
    head_of = lax.broadcasted_iota(jnp.int32, (WQ, channels), 1) // head_width
    lane = lax.broadcasted_iota(jnp.int32, (1, WK), 1)
    scale = 1.0 / math.sqrt(head_width)

    def windows(step, carry):
        scores = []
        bases = [pl.multiple_of(step * (BATCH * WQ) + i * WQ, WQ) for i in range(BATCH)]
        for i, base in enumerate(bases):
            queries = query_ref[pl.ds(base, WQ), :]
            stacked = jnp.concatenate(
                [jnp.where(head_of == head, queries, 0).astype(jnp.bfloat16) for head in range(HA)],
                axis=0,
            )
            score = lax.dot_general(
                stacked, key_ref[pl.ds(base, WK), :], (((1,), (1,)), ((), ())),
                preferred_element_type=jnp.float32,
            )
            bias = bias_ref[:, pl.ds(base, WQ), :].reshape(HA * WQ, WK).astype(jnp.float32)
            slot = first_ref[0] + base - RIM + lane
            index = step * BATCH + i
            inside = (slot >= bounds_ref[2 * index]) & (slot < bounds_ref[2 * index + 1])
            scores.append(jnp.where(inside, score * scale + bias, FAR))
        weights = [jnp.exp(score - jnp.max(score, axis=-1, keepdims=True)) for score in scores]
        results = []
        for base, weight in zip(bases, weights):
            attended = matmul(weight.astype(jnp.bfloat16), value_ref[pl.ds(base, WK), :])
            attended = attended / jnp.sum(weight, axis=-1, keepdims=True)
            result = jnp.zeros((WQ, channels), jnp.float32)
            for head in range(HA):
                result = result + jnp.where(
                    head_of == head, attended[head * WQ : (head + 1) * WQ], 0.0
                )
            results.append(result)
        start = pl.multiple_of(step * (BATCH * WQ), BATCH * WQ)
        held_ref[pl.ds(start, BATCH * WQ), :] = jnp.concatenate(results, axis=0)
        return carry

    lax.fori_loop(0, count // (BATCH * WQ), windows, 0)
    gated = (held_ref[...] * jax.nn.sigmoid(gate_ref[...].astype(jnp.float32))).astype(jnp.bfloat16)
    fresh = state_ref[inner, :] + matmul(gated, weight_ref[6])
    final = layer_norm(fresh).astype(jnp.bfloat16)
    out_ref[...] = lax.dot_general(
        position_ref[...], final, (((1,), (1,)), ((), ())), preferred_element_type=jnp.float32
    )


BATCH = 8


def atom_block(first, bounds, rows, skip, cond, rims, owners, weights, vectors, positions, bias):
    count, channels = bias.shape[1], skip.shape[1]
    extended = skip.shape[0] + 2 * RIM
    smem = pl.BlockSpec(memory_space=pltpu.SMEM)
    vmem = pl.BlockSpec(memory_space=pltpu.VMEM)
    return pl.pallas_call(
        atom_kernel,
        in_specs=[smem, smem] + [vmem] * 9,
        out_specs=vmem,
        out_shape=jax.ShapeDtypeStruct((positions.shape[0], count), jnp.float32),
        scratch_shapes=[
            pltpu.VMEM((extended, channels), jnp.float32),
            pltpu.VMEM((count, channels), jnp.bfloat16),
            pltpu.VMEM((count, channels), jnp.bfloat16),
            pltpu.VMEM((extended, channels), jnp.bfloat16),
            pltpu.VMEM((extended, channels), jnp.bfloat16),
            pltpu.VMEM((count, channels), jnp.float32),
        ],
        compiler_params=pltpu.CompilerParams(vmem_limit_bytes=VMEM_LIMIT),
        name="atom_block",
    )(first, bounds, rows, skip, cond, rims, owners, weights, vectors, positions, bias)


def rims(array):
    return jnp.stack([array[:RIM], array[array.shape[0] - RIM :]])


def per_device(
    token_act,
    token_cond,
    pair_bias,
    token_mask,
    ada_weights,
    attention_in,
    attention_out,
    transition_in,
    transition_out,
    token_vectors,
    atom_skip,
    atom_cond,
    atom_bias,
    window_bounds,
    atom_token,
    atom_weights,
    token_to_atom,
    atom_vectors,
    position_out,
):
    groups = lax.axis_size("fsdp")
    act_rows = token_act[0]
    row_count, depth = act_rows.shape
    column_count = attention_in.shape[2]
    channels = atom_cond.shape[1]
    start = lax.axis_index("fsdp") * column_count
    atom_rims = rims(jnp.concatenate([atom_skip[0], atom_cond], axis=1))
    owner_rims = jnp.pad(rims(atom_token)[:, None, :], ((0, 0), (0, 0), (0, 2 * WK - RIM)))
    small = jnp.concatenate([atom_weights.reshape(-1, channels), token_to_atom], axis=0)
    small_height = small.shape[0] // 2
    small_half = lax.dynamic_slice_in_dim(
        small, lax.rem(lax.axis_index("seq"), 2) * small_height, small_height
    )

    cond_normed = layer_norm(token_cond[0]).astype(jnp.bfloat16)
    act_normed = layer_norm(act_rows).astype(jnp.bfloat16)
    act_slots = jnp.transpose(act_normed.reshape(row_count, groups, column_count), (1, 0, 2))
    cond_all, act_all, atom_rims, owner_rims = move(
        1,
        (
            ("line", "fsdp", cond_normed, 4),
            ("exchange", "fsdp", pack(act_slots), 1),
            ("halo", "seq", atom_rims, 1),
            ("halo", "seq", owner_rims, 1),
        ),
    )
    owners = jnp.concatenate([owner_rims[0, 0, :RIM], atom_token, owner_rims[1, 0, :RIM]])[:, None]
    cond_flat = cond_all.reshape(groups * row_count, depth)
    act_flat = unpack(act_all).reshape(groups * row_count, column_count).astype(jnp.float32)

    def adaptive(scale_index, shift_index, vector_index):
        offset = lax.dynamic_slice_in_dim(token_vectors[vector_index], start, column_count)
        scaled = jax.nn.sigmoid(matmul(cond_flat, ada_weights[scale_index]) + offset) * act_flat
        rows = (scaled + matmul(cond_flat, ada_weights[shift_index])).astype(jnp.bfloat16)
        return pack(rows.reshape(groups, row_count, column_count))

    def joined(array):
        array = unpack(array)
        return jnp.transpose(array, (1, 2, 0, 3)).reshape(groups * row_count, depth)

    attend_all, small_halves = move(
        2, (("line", "fsdp", adaptive(0, 1, 0), groups), ("line", "fsdp", small_half, 1))
    )
    transit_part = adaptive(2, 3, 1)
    attend_flat = joined(attend_all)
    query_bias = lax.dynamic_slice_in_dim(token_vectors[2], start, column_count)

    def project(index):
        return matmul(attend_flat, attention_in[index])

    def grouped(array):
        return array.astype(jnp.bfloat16).reshape(groups, row_count, -1)

    keys_values = jnp.concatenate([grouped(project(1)), grouped(project(2))], axis=-1)
    kv_all, transit_all, mask_all, small_all = move(
        3,
        (
            ("paired", "seq", keys_values, groups),
            ("line", "fsdp", transit_part, groups),
            ("paired", "seq", token_mask[None], 1),
            ("swap", "seq", small_halves, 1),
        ),
    )
    small_all = jnp.transpose(small_all, (1, 0, 2, 3)).reshape(groups, -1, channels)
    query_rows = grouped(project(0) + query_bias)
    gate_rows = grouped(project(3))
    weight_rows = atom_weights.size // channels
    atom_full = jnp.transpose(
        small_all[:, :weight_rows].reshape((groups,) + atom_weights.shape), (1, 2, 0, 3)
    ).reshape(atom_weights.shape[0], channels, channels)
    project_full = small_all[:, weight_rows:].reshape(depth, channels)
    gated = token_attention(
        query_rows, gate_rows, kv_all, pair_bias, mask_all.reshape(1, -1)
    ).reshape(groups * row_count, -1)
    transit_flat = joined(transit_all)
    hidden = (
        jax.nn.silu(matmul(transit_flat, transition_in[0])) * matmul(transit_flat, transition_in[1])
    ).astype(jnp.bfloat16)
    partial_sum = matmul(gated, attention_out) + matmul(hidden, transition_out)
    token_result, all_rows = close(
        4,
        "fsdp",
        "seq",
        partial_sum.astype(jnp.bfloat16).reshape(groups, row_count, depth),
        act_rows,
        project_full,
    )
    first_atom = (lax.axis_index("seq") * atom_cond.shape[0]).astype(jnp.int32).reshape(1)
    update = atom_block(
        first_atom,
        window_bounds.reshape(-1),
        all_rows.reshape(-1, channels),
        atom_skip[0],
        atom_cond,
        atom_rims,
        owners,
        atom_full,
        atom_vectors,
        position_out,
        atom_bias,
    )
    return (token_result[None], update[None])


def solution(mesh):
    in_specs = (
        P(("sample", "fsdp"), "seq", None),
        P(("sample", "fsdp"), "seq", None),
        P("fsdp", "seq", None),
        P("seq"),
        P(None, None, "fsdp"),
        P(None, None, "fsdp"),
        P("fsdp", None),
        P(None, None, "fsdp"),
        P("fsdp", None),
        P(),
        P(("sample", "fsdp"), "seq", None),
        P("seq", None),
        P(None, "seq", None),
        P("seq", None),
        P("seq"),
        P(None, None, "fsdp"),
        P("fsdp", None),
        P(),
        P(),
    )
    out_specs = (P(("sample", "fsdp"), "seq", None), P(("sample", "fsdp"), None, "seq"))
    return jax.shard_map(
        per_device, mesh=mesh, in_specs=in_specs, out_specs=out_specs, check_vma=False
    )
```

profile of v0, /device:TPU:0, one launch (start us, length us, event | category | flops | bytes accessed | tf_op | source)
XLA Modules:
  0.0 145.2 jit_solution(5804265202366672812)
XLA Ops:
  0.7 1.1 convert_reduce_fusion.1
  1.8 1.1 fusion.43
  2.9 1.8 %fusion.44.refs_0_ = bf16[128,768]{1,0:T(8,128)(2,1)} fusion(bf16[1,128,768]{2,1,0:T(8,128)(2,1)} %param.20, f32[128]{0:T(128)S(1)} %add_rsqrt_fusion.1, f32[128]{0:T(128)S(1)} %broadcast_multiply_fusion.1), kind=kLoop, calls=%fused_computation.57 | loop fusion | flops 393216 | bytes 394240 | tf_op jit(solution)/shard_map/convert_element_type | solution.py:660
  4.7 1.1 copy.53
  8.6 24.8 %move1.1 = (bf16[4,128,768]{2,1,0:T(8,128)(2,1)}, bf16[4,64,384]{2,1,0:T(8,128)(2,1)}, bf16[2,48,256]{2,1,0:T(8,128)(2,1)}, s32[2,1,256]{2,1,0:T(1,128)}) custom-call(bf16[128,768]{1,0:T(8,128)(2,1)} %fusion.44.refs_0_, bf16[4,64,384]{2,1,0:T(8,128)(2,1)} %pad_maximum_fusion.2.refs_1_, bf16[2,48,256]{2,1,0:T(8,128)(2,1)} %pad_maximum_fusion.5.refs_2_, ...), custom_call_target="tpu_custom_call" | custom-call | bytes 13332480 | tf_op jit(solution)/shard_map/move1/pallas_call | solution.py:392
  33.4 1.1 fusion.73
  39.2 20.6 %move2.1 = (bf16[4,4,64,384]{3,2,1,0:T(8,128)(2,1)}, bf16[4,208,128]{2,1,0:T(8,128)(2,1)}) custom-call(bf16[4,64,384]{2,1,0:T(8,128)(2,1)} %pad_maximum_fusion.3.refs_0_, bf16[208,128]{1,0:T(8,128)(2,1)} %fusion.65.refs_1_), custom_call_target="tpu_custom_call" | custom-call | bytes 7495680 | tf_op jit(solution)/shard_map/move2/pallas_call | solution.py:392
  59.8 1.5 %fusion.69 = (bf16[4,4,64,192]{3,2,1,0:T(8,128)(2,1)S(1)}, bf16[4,4,64,192]{3,2,1,0:T(8,128)(2,1)S(1)}) fusion(bf16[4,4,64,384]{3,2,1,0:T(8,128)(2,1)} %get-tuple-element.16), kind=kLoop, calls=%fused_computation.105 | loop fusion | bytes 1572864 | tf_op jit(solution)/shard_map/slice | solution.py:40
  62.2 1.4 fusion.13
  66.1 1.3 convolution_convert_fusion.1
  67.5 0.9 pad_maximum_fusion.refs_0_
  68.4 1.4 fusion.5
  69.9 1.4 fusion.12
  72.2 21.7 %move3.1 = (bf16[4,4,128,384]{3,2,1,0:T(8,128)(2,1)}, bf16[4,4,64,384]{3,2,1,0:T(8,128)(2,1)}, s32[4,1,128]{2,1,0:T(1,128)}, bf16[2,4,208,128]{3,2,1,0:T(8,128)(2,1)}) custom-call(bf16[4,128,384]{2,1,0:T(8,128)(2,1)} %pad_maximum_fusion.refs_0_, bf16[4,64,384]{2,1,0:T(8,128)(2,1)} %pad_maximum_fusion.4.refs_1_, s32[1,128]{1,0:T(1,128)} %bitcast.162, ...), custom_call_target="tpu_custom_call" | custom-call | bytes 24099840 | tf_op jit(solution)/shard_map/move3/pallas_call | solution.py:392
  93.9 5.7 %token_attention.1 = bf16[4,128,192]{2,1,0:T(8,128)(2,1)} custom-call(bf16[4,128,192]{2,1,0:T(8,128)(2,1)} %bitcast.134, bf16[4,128,192]{2,1,0:T(8,128)(2,1)} %bitcast.135, bf16[4,4,128,384]{3,2,1,0:T(8,128)(2,1)} %get-tuple-element.18.kv_ref, bf16[4,128,512]{2,1,0:T(8,128)(2,1)} %bias_ref.2, s32[1,512]{1,0:T(1,128)} %bitcast.158), custom_call_target="tpu_custom_call" | custom-call | tf_op jit(solution)/shard_map/token_attention/pallas_call | solution.py:503
  99.7 1.4 fusion.75
  101.5 1.3 copy.67
  102.9 2.9 %fusion.16 = f32[512,384]{1,0:T(8,128)} fusion(bf16[96,8,4,128]{3,2,1,0:T(4,128)(2,1)} %bitcast.148, bf16[2,768,384]{2,1,0:T(8,128)(2,1)} %param.26), kind=kOutput, calls=%fused_computation.27 | convolution fusion | flops 301989888 | bytes 2162688 | tf_op jit(solution)/shard_map/dot_general | solution.py:30
  105.8 3.4 %add_convert_fusion = bf16[512,768]{1,0:T(8,128)(2,1)} fusion(f32[512,768]{1,0:T(8,128)S(1)} %fusion.75, bf16[384,768]{1,0:T(8,128)(2,1)S(1)} %copy-done, f32[512,384]{1,0:T(8,128)} %fusion.16, bf16[96,8,4,128]{3,2,1,0:T(4,128)(2,1)S(1)} %bitcast.149, bf16[2,768,384]{2,1,0:T(8,128)(2,1)} %param.26), kind=kOutput, calls=%fused_computation | convolution fusion | flops 605945856 | bytes 5111808 | tf_op jit(solution)/shard_map/dot_general | solution.py:30
  109.9 23.3 %close.1 = (bf16[128,768]{1,0:T(8,128)(2,1)}, bf16[4,128,128]{2,1,0:T(8,128)(2,1)}) custom-call(bf16[4,128,768]{2,1,0:T(8,128)(2,1)} %bitcast.151, bf16[128,768]{1,0:T(8,128)(2,1)} %bitcast.131, bf16[768,128]{1,0:T(8,128)(2,1)} %bitcast.150), custom_call_target="tpu_custom_call" | custom-call | tf_op jit(solution)/shard_map/close/pallas_call | solution.py:431
  134.0 1.0 broadcast_in_dim.27.token_ref
  135.7 0.8 copy.72.weight_ref
  136.6 6.6 %atom_block.1 = f32[3,1024]{1,0:T(4,128)} custom-call(s32[1]{0:T(128)} %bitcast.43.first_ref, s32[64]{0:T(128)} %reshape.128.bounds_ref, bf16[512,128]{1,0:T(8,128)(2,1)} %bitcast.155, bf16[1024,128]{1,0:T(8,128)(2,1)} %bitcast.141, bf16[1024,128]{1,0:T(8,128)(2,1)} %cond_ref.1, bf16[2,48,256]{2,1,0:T(8,128)(2,1)} %get-tuple-element.24.rim_ref, ...), custom_call_target="tpu_custom_call" | custom-call | tf_op jit(solution)/shard_map/atom_block/pallas_call | solution.py:603
  143.2 1.3 copy.73
  (92 shorter events, 15.2 us)
Async XLA Ops:
  0.6 105.1 %copy-start = (bf16[384,768]{1,0:T(8,128)(2,1)S(1)}, bf16[384,768]{1,0:T(8,128)(2,1)}, u32[]{:S(2)}) copy-start(bf16[384,768]{1,0:T(8,128)(2,1)} %param.27) | copy-start | bytes 1769476
  0.6 5.3 %copy-start.2 = (bf16[1,128,768]{2,1,0:T(8,128)(2,1)S(1)}, bf16[1,128,768]{2,1,0:T(8,128)(2,1)}, u32[]{:S(2)}) copy-start(bf16[1,128,768]{2,1,0:T(8,128)(2,1)} %param.19) | copy-start | bytes 589828
  5.9 1.3 copy-start.4
  6.0 1.3 copy-start.5
  6.3 1.6 %copy-start.16 = (s32[1024]{0:T(1024)S(1)}, s32[1024]{0:T(1024)}, u32[]{:S(2)}) copy-start(s32[1024]{0:T(1024)} %param.33) | copy-start | bytes 12292
  34.5 0.7 copy-start.15
  34.5 1.1 copy-start.1
  34.5 1.7 %copy-start.10 = (bf16[4,768,192]{1,2,0:T(8,128)(2,1)S(1)}, bf16[4,768,192]{1,2,0:T(8,128)(2,1)}, u32[]{:S(2)}) copy-start(bf16[4,768,192]{1,2,0:T(8,128)(2,1)} %param.23) | copy-start | bytes 3538948
  34.8 1.8 %copy-start.8 = (f32[512,192]{0,1:T(8,128)}, f32[512,192]{0,1:T(8,128)S(1)}, u32[]{:S(2)}) copy-start(f32[512,192]{0,1:T(8,128)S(1)} %copy.57) | copy-start | bytes 1179652
  36.6 1.4 copy-start.13
  37.1 1.3 copy-start.14
  62.1 2.3 %copy-start.19 = (bf16[4,768,192]{1,2,0:T(8,128)(2,1)S(1)}, bf16[4,768,192]{1,2,0:T(8,128)(2,1)}, u32[]{:S(2)}) copy-start(bf16[4,768,192]{1,2,0:T(8,128)(2,1)} %param.24) | copy-start | bytes 3538948
  66.0 2.4 %copy-start.9 = (f32[512,192]{0,1:T(8,128)S(1)}, f32[512,192]{0,1:T(8,128)}, u32[]{:S(2)}) copy-start(f32[512,192]{0,1:T(8,128)} %copy-done.8) | copy-start | bytes 1179652
  93.9 5.7 %copy-start.11 = (bf16[192,768]{1,0:T(8,128)(2,1)S(1)}, bf16[192,768]{1,0:T(8,128)(2,1)}, u32[]{:S(2)}) copy-start(bf16[192,768]{1,0:T(8,128)(2,1)} %param.25) | copy-start | bytes 884740
  99.6 1.4 copy-start.3
  102.9 2.9 %copy-start.6 = (bf16[4,128,4,192]{1,0,3,2:T(4,128)(2,1)S(1)}, bf16[4,128,4,192]{1,0,3,2:T(4,128)(2,1)}, u32[]{:S(2)}) copy-start(bf16[4,128,4,192]{1,0,3,2:T(4,128)(2,1)} %copy.67) | copy-start | bytes 2359300
  105.8 3.4 %copy-start.7 = (bf16[2,4,208,128]{3,2,1,0:T(8,128)(2,1)S(1)}, bf16[2,4,208,128]{3,2,1,0:T(8,128)(2,1)}, u32[]{:S(2)}) copy-start(bf16[2,4,208,128]{3,2,1,0:T(8,128)(2,1)} %get-tuple-element.21) | copy-start | bytes 1277956
  109.2 24.0 %copy-start.17 = (s32[32,2]{0,1:T(2,128)S(1)}, s32[32,2]{0,1:T(2,128)}, u32[]{:S(2)}) copy-start(s32[32,2]{0,1:T(2,128)} %param.32) | copy-start | bytes 772
  109.2 24.7 %copy-start.18 = (s32[2,1,256]{2,1,0:T(1,128)S(1)}, s32[2,1,256]{2,1,0:T(1,128)}, u32[]{:S(2)}) copy-start(s32[2,1,256]{2,1,0:T(1,128)} %get-tuple-element.25) | copy-start | bytes 6148
  136.6 7.9 %copy-start.12 = (bf16[128,768]{1,0:T(8,128)(2,1)S(1)}, bf16[128,768]{1,0:T(8,128)(2,1)}, u32[]{:S(2)}) copy-start(bf16[128,768]{1,0:T(8,128)(2,1)} %get-tuple-element.22) | copy-start | bytes 589828
where the time goes:
time: 148 us; the launch traced here: 145 us
  Pallas kernels  103 us (70%)
  local copies, waits for them, and re-layouts  17.1 us (12%)
  matrix products  14.7 us (10%)
  other arithmetic  9.65 us (7%)
    pallas_call x3, Pallas kernels, move(): pl.pallas_call(functools.partial(move_kernel, tuple(kinds)), out_shape=tu...  67.1 us
    pallas_call x1, Pallas kernels, close(): pl.pallas_call(functools.partial(close_kernel, axis, size, row_axis, row_...  23.3 us
    dot_general x11, matrix products, matmul(): return jnp.dot(left_side, right_side, preferred_element_type=jnp.float32)  14.7 us
    pallas_call x1, Pallas kernels, atom_block(): pl.pallas_call(atom_kernel, in_specs=[smem, smem] + [vmem] * 9, out_specs...  6.58 us
    pallas_call x1, Pallas kernels, token_attention(): pl.pallas_call(functools.partial(attention_kernel, heads, max(512 // piec...  5.7 us
    unnamed x45, local copies, waits for them, and re-layouts  4.69 us

commit v1 on v0

v1 whole, which is shorter than its diff:
```python
import functools
import math
import types

import jax
import jax.numpy as jnp
from jax import lax
from jax.experimental import pallas as pl
from jax.experimental.pallas import tpu as pltpu
from jax.sharding import PartitionSpec as P

HA = 4
WQ = 32
WK = 128
HD = 48
EPS = 1e-05
FAR = -1e30
RIM = (WK - WQ) // 2
VMEM_LIMIT = 56 * 1024 * 1024
MESH = pl.DeviceIdType.MESH


def layer_norm(values):
    values = values.astype(jnp.float32)
    center = values - jnp.mean(values, axis=-1, keepdims=True)
    spread = jnp.mean(center * center, axis=-1, keepdims=True)
    return center * lax.rsqrt(spread + EPS)


def matmul(left_side, right_side):
    return jnp.dot(left_side, right_side, preferred_element_type=jnp.float32)


def matmul_t(left_side, right_side):
    return lax.dot_general(
        left_side, right_side, (((1,), (1,)), ((), ())), preferred_element_type=jnp.float32
    )


def pack(array):
    half = array.shape[-2] // 2
    return jnp.concatenate([array[..., :half, :], array[..., half:, :]], axis=-1)


def unpack(array):
    half = array.shape[-1] // 2
    return jnp.concatenate([array[..., :half], array[..., half:]], axis=-2)


def remote(source, target, send, recv, axis, peer):
    return pltpu.make_async_remote_copy(
        src_ref=source, dst_ref=target, send_sem=send, recv_sem=recv,
        device_id={axis: peer}, device_id_type=MESH,
    )


class Chain:
    def __init__(self, axis, size, view, send, recv, prefix):
        self.axis, self.size, self.view = axis, size, view
        self.send, self.recv, self.prefix = send, recv, prefix
        self.here = lax.axis_index(axis)

    def guards(self, side, step):
        here, last = self.here, self.size - 1
        if side == 0:
            return (here - step >= 0) & (here < last), here - 1 - step >= 0
        return (here + step <= last) & (here > 0), here + 1 + step <= last

    def copy(self, side, step, arriving):
        sign = 1 if side == 0 else -1
        block = self.view(self.here - sign * (step + (1 if arriving else 0)))
        at = self.prefix + (side, step)
        return remote(block, block, self.send.at[at], self.recv.at[at], self.axis, self.here + sign)

    def begin(self):
        for side in (0, 1):

            @pl.when(self.guards(side, 0)[0])
            def _():
                self.copy(side, 0, False).start()

    def arrive(self, step):
        for side in (0, 1):
            comes = self.guards(side, step)[1]

            @pl.when(comes)
            def _():
                self.copy(side, step, True).wait_recv()

            if step + 1 < self.size - 1:

                @pl.when(self.guards(side, step + 1)[0])
                def _():
                    self.copy(side, step + 1, False).start()

    def drain(self):
        for side in (0, 1):
            for step in range(self.size - 1):

                @pl.when(self.guards(side, step)[0])
                def _():
                    self.copy(side, step, False).wait_send()


class Pairs:
    def __init__(self, axis, size, view, send, recv, partner_send, partner_recv, prefix):
        self.axis, self.view, self.prefix = axis, view, prefix
        self.send, self.recv = send, recv
        self.partner_send, self.partner_recv = partner_send, partner_recv
        self.index = lax.axis_index(axis)
        self.length = size // 2
        self.position = self.index // 2
        self.parity = self.index - 2 * self.position

    def slot(self, position):
        return position * 2 + self.parity

    def partner(self):
        return self.index + 1 - 2 * self.parity

    def guards(self, side, step):
        here, last = self.position, self.length - 1
        if side == 0:
            return (here - step >= 0) & (here < last), here - 1 - step >= 0
        return (here + step <= last) & (here > 0), here + 1 + step <= last

    def copy(self, side, step, arriving):
        sign = 1 if side == 0 else -1
        block = self.view(self.slot(self.position - sign * (step + (1 if arriving else 0))))
        at = self.prefix + (side, step)
        return remote(
            block, block, self.send.at[at], self.recv.at[at], self.axis,
            self.slot(self.position + sign),
        )

    def hand(self, key, origin, arriving):
        block = self.view(origin * 2 + 1 - self.parity if arriving else self.slot(origin))
        at = self.prefix + (key,)
        return remote(
            block, block, self.partner_send.at[at], self.partner_recv.at[at], self.axis, self.partner()
        )

    def greet(self, signal):
        above, below = self.position > 0, self.position < self.length - 1

        @pl.when(above)
        def _():
            signal(self.axis, self.slot(self.position - 1))

        @pl.when(below)
        def _():
            signal(self.axis, self.slot(self.position + 1))

        signal(self.axis, self.partner())
        return jnp.where(above, 1, 0) + jnp.where(below, 1, 0) + 1

    def begin(self):
        for side in (0, 1):

            @pl.when(self.guards(side, 0)[0])
            def _():
                self.copy(side, 0, False).start()

        self.hand(0, self.position, False).start()

    def key(self, side, step):
        return 1 + side * (self.length - 1) + step

    def origin(self, side, step):
        return self.position - (step + 1) if side == 0 else self.position + step + 1

    def relay(self):
        for step in range(self.length - 1):
            for side in (0, 1):

                @pl.when(self.guards(side, step)[1])
                def _():
                    self.copy(side, step, True).wait_recv()
                    self.hand(self.key(side, step), self.origin(side, step), False).start()

                if step + 1 < self.length - 1:

                    @pl.when(self.guards(side, step + 1)[0])
                    def _():
                        self.copy(side, step + 1, False).start()

    def complete(self):
        self.hand(0, self.position, False).wait_send()
        self.hand(0, self.position, True).wait_recv()
        for step in range(self.length - 1):
            for side in (0, 1):
                goes, comes = self.guards(side, step)

                @pl.when(goes)
                def _():
                    self.copy(side, step, False).wait_send()

                @pl.when(comes)
                def _():
                    self.hand(self.key(side, step), self.origin(side, step), False).wait_send()
                    self.hand(self.key(side, step), self.origin(side, step), True).wait_recv()


def token_kernel(names, groups, ring, *refs):
    r = types.SimpleNamespace(**dict(zip(names, refs)))
    me, seat = lax.axis_index("fsdp"), lax.axis_index("seq")
    rows, depth = r.act.shape
    width = r.ada.shape[1]
    heads = r.bias.shape[0]
    half = rows // 2
    last = groups - 1
    barrier = pltpu.get_barrier_semaphore()

    def signal(axis, target):
        pl.semaphore_signal(barrier, inc=1, device_id={axis: target}, device_id_type=MESH)

    loads = {
        name: pltpu.make_async_copy(getattr(r, name + "_hbm"), getattr(r, name), r.load.at[number])
        for number, name in enumerate(("ada", "attn", "bias", "out", "tin", "tout"))
    }

    def pairs(view, *prefix):
        return Pairs("seq", ring, view, r.seq_send, r.seq_recv, r.hand_send, r.hand_recv, prefix)

    halos = [
        Halo("seq", ring, r.rim, r.rim_all, r.halo_send.at[0], r.halo_recv.at[0]),
        Halo("seq", ring, r.owner, r.owner_all, r.halo_send.at[1], r.halo_recv.at[1]),
    ]
    kv_flows = [pairs(lambda slot, g=g: r.kv.at[slot, g], g) for g in range(groups)]
    mask_flow = pairs(lambda slot: r.masks.at[slot], groups)
    rows_flow = pairs(lambda slot: r.rows_all.at[slot], groups + 1)

    for shift in range(1, groups):
        signal("fsdp", lax.rem(me + shift, groups))
    expected = last + mask_flow.greet(signal) + halos[0].greet(barrier)
    for load in loads.values():
        load.start()

    def chain(number, view):
        return Chain("fsdp", groups, view, r.line_send, r.line_recv, (number,))

    cond_chains = [
        chain(part, lambda slot, part=part: r.conds.at[slot, pl.ds(part * half, half)]) for part in (0, 1)
    ]
    attend_chains = [chain(2 + g, lambda slot, g=g: r.attend.at[slot, g]) for g in range(groups)]
    transit_chains = [
        chain(2 + groups + g, lambda slot, g=g: r.transit.at[slot, g]) for g in range(groups)
    ]
    parity = seat - 2 * (seat // 2)
    atom_half, project_half = r.atom_part.shape[0] // 2, r.project_part.shape[0] // 2
    atom_rows = pl.ds(pl.multiple_of(parity * atom_half, 16), atom_half)
    project_rows = pl.ds(pl.multiple_of(parity * project_half, 16), project_half)
    small_chains = [
        chain(2 + 2 * groups, lambda slot: r.atom_all.at[slot, atom_rows]),
        chain(3 + 2 * groups, lambda slot: r.project.at[slot, project_rows]),
    ]

    def swaps():
        partner = seat + 1 - 2 * parity
        blocks = (r.atom_all.at[:, atom_rows], r.project.at[:, project_rows])
        return [
            remote(block, block, r.swap_send.at[i], r.swap_recv.at[i], "seq", partner)
            for i, block in enumerate(blocks)
        ]

    r.conds[me] = layer_norm(r.cond[...]).astype(jnp.bfloat16)
    r.masks[seat] = r.mask[...]
    r.atom_all[me, atom_rows] = r.atom_part[atom_rows, :]
    r.project[me, project_rows] = r.project_part[project_rows, :]
    pl.semaphore_wait(barrier, expected)
    for flow in cond_chains:
        flow.begin()
    act_normed = layer_norm(r.act[...]).astype(jnp.bfloat16)
    for g in range(groups):
        r.act_out[g] = pack(act_normed[:, g * width : (g + 1) * width])

    def slots(shift, arriving):
        peer = lax.rem(me + shift, groups)
        landing = lax.rem(me + groups - shift, groups) if arriving else me
        return remote(
            r.act_out.at[peer], r.acts.at[landing], r.act_send.at[shift], r.act_recv.at[shift],
            "fsdp", peer,
        )

    for shift in range(1, groups):
        slots(shift, False).start()
    mask_flow.begin()
    for halo in halos:
        halo.begin()
    offsets = r.vectors[me]

    def adaptive(sample, packed):
        rows_in = r.conds[sample]
        values = unpack(packed).astype(jnp.float32)

        def one(scale, shift, vector):
            gate = jax.nn.sigmoid(matmul_t(rows_in, r.ada[scale]) + offsets[vector : vector + 1, :])
            return pack((gate * values + matmul_t(rows_in, r.ada[shift])).astype(jnp.bfloat16))

        r.attend[me, sample] = one(0, 1, 0)
        r.transit[me, sample] = one(2, 3, 1)

    loads["ada"].wait()
    adaptive(me, r.act_out[me])
    inner = sorted(range(groups), key=lambda g: max(g, last - g))
    outer = sorted(range(groups), key=lambda g: (-max(g, last - g), g))
    for step in range(last):
        for flow in cond_chains:
            flow.arrive(step)
        for side in (0, 1):

            @pl.when(cond_chains[0].guards(side, step)[1])
            def _():
                origin = me - (step + 1) if side == 0 else me + step + 1
                slots(step + 1 if side == 0 else last - step, True).wait_recv()
                adaptive(origin, r.acts[origin])

        for g in inner:
            if max(g, last - g) == step + 1:
                attend_chains[g].begin()

    def joined(ref, g):
        return jnp.concatenate([unpack(ref[origin, g]) for origin in range(groups)], axis=1)

    def projections(g):
        full = joined(r.attend, g)
        r.queries[g] = (matmul_t(full, r.attn[0]) + offsets[2:3, :]).astype(jnp.bfloat16)
        both = r.attn[1:3].reshape(2 * width, depth)
        r.kv[seat, g] = matmul_t(full, both).astype(jnp.bfloat16)
        kv_flows[g].begin()
        r.gates[g] = matmul_t(full, r.attn[3]).astype(jnp.bfloat16)

    for step in range(last - 1):
        for g in inner:
            attend_chains[g].arrive(step)
    for g in outer:
        transit_chains[g].begin()
    loads["attn"].wait()
    for g in inner:
        attend_chains[g].arrive(last - 1)
        projections(g)
    for flow in small_chains:
        flow.begin()

    def attention(g):
        queries = r.queries[g]
        head_of = lax.broadcasted_iota(jnp.int32, (rows, width), 1) // HD
        stacked = jnp.concatenate(
            [jnp.where(head_of == head, queries, 0).astype(jnp.bfloat16) for head in range(heads)], axis=0
        )
        scale = 1.0 / math.sqrt(HD)
        span = min(max(512 // rows, 1), ring)

        def block(first, state):
            keys = jnp.concatenate([r.kv[first + i, g, :, :width] for i in range(span)], axis=0)
            values = jnp.concatenate([r.kv[first + i, g, :, width:] for i in range(span)], axis=0)
            live = jnp.concatenate([r.masks[first + i] for i in range(span)], axis=1)
            columns = pl.ds(pl.multiple_of(first * rows, span * rows), span * rows)
            bias = r.bias[:, :, columns].reshape(heads * rows, span * rows).astype(jnp.float32)
            scores = matmul_t(stacked, keys) * scale + bias
            scores = jnp.where(live > 0, scores, FAR)
            block_max = jnp.max(scores, axis=-1, keepdims=True)
            new_maxima = block_max if state is None else jnp.maximum(state[0], block_max)
            weights = jnp.exp(scores - new_maxima)
            totals = jnp.sum(weights, axis=-1, keepdims=True)
            summed = matmul(weights.astype(jnp.bfloat16), values)
            if state is not None:
                factor = jnp.exp(state[0] - new_maxima)
                totals, summed = state[1] * factor + totals, state[2] * factor + summed
            return new_maxima, totals, summed

        state = block(0, None)
        if ring > span:
            state = lax.fori_loop(1, ring // span, lambda i, state: block(i * span, state), state)
        attended = state[2] / state[1]
        result = jnp.zeros((rows, width), jnp.float32)
        for head in range(heads):
            result = result + jnp.where(head_of == head, attended[head * rows : (head + 1) * rows], 0.0)
        gate = jax.nn.sigmoid(r.gates[g].astype(jnp.float32))
        r.gated[g] = (result * gate).astype(jnp.bfloat16)

    pending = [(transit_chains[g], step) for step in range(last - 1) for g in outer]
    pending += [(flow, step) for step in range(last - 1) for flow in small_chains]
    share = -(-len(pending) // groups)
    mask_flow.relay()
    mask_flow.complete()
    loads["bias"].wait()
    kv_flows[inner[0]].relay()
    for number, g in enumerate(inner):
        if number + 1 < groups:
            kv_flows[inner[number + 1]].relay()
        kv_flows[g].complete()
        attention(g)
        for flow, step in pending[number * share : (number + 1) * share]:
            flow.arrive(step)

    def hop(side, g, part):
        piece = pl.ds(part * half, half)
        at = (side, g, part)
        return remote(
            r.sums_out.at[g, piece], r.sums_in.at[side, g, piece], r.sum_send.at[at], r.sum_recv.at[at],
            "fsdp", me + (1 if side == 0 else -1),
        )

    def take(side, g, part):
        hop(side, g, part).wait_recv()
        piece = pl.ds(part * half, half)
        r.total[g, piece] += r.sums_in[side, g, piece].astype(jnp.float32)

    def reduce(stage, g):
        for side, here, goes in ((0, stage, g > stage), (1, last - stage, g < last - stage)):
            if goes:

                @pl.when(me == here)
                def _():
                    for part in (0, 1):
                        piece = pl.ds(part * half, half)
                        if stage > 0:
                            take(side, g, part)
                        r.sums_out[g, piece] = r.total[g, piece].astype(jnp.bfloat16)
                        hop(side, g, part).start()

    for name in ("out", "tin", "tout"):
        loads[name].wait()
    for g in outer:
        transit_chains[g].arrive(last - 1)
        full = joined(r.transit, g)
        hidden = jax.nn.silu(matmul(full, r.tin[0])) * matmul(full, r.tin[1])
        r.total[g] = matmul(r.gated[g], r.out[...]) + matmul(hidden.astype(jnp.bfloat16), r.tout[...])
        reduce(0, g)
    for flow in small_chains:
        flow.arrive(last - 1)
    for copy in swaps():
        copy.start()
    for stage in range(1, last):
        for g in outer:
            reduce(stage, g)
    for copy in swaps():
        copy.wait()
    for side, present in ((0, me > 0), (1, me < last)):

        @pl.when(present)
        def _():
            for part in (0, 1):
                take(side, me, part)

    token = (r.act[...].astype(jnp.float32) + r.total[me]).astype(jnp.bfloat16)
    r.token[...] = token
    r.rows_all[seat] = matmul(token, r.project[...].reshape(depth, -1)).astype(jnp.bfloat16)
    rows_flow.begin()
    for flow in cond_chains + attend_chains + transit_chains + small_chains:
        flow.drain()
    for shift in range(1, groups):
        slots(shift, False).wait_send()
    for halo in halos:
        halo.finish()
    for g in range(groups):
        for side, goes in ((0, g > me), (1, g < me)):

            @pl.when(goes)
            def _():
                for part in (0, 1):
                    hop(side, g, part).wait_send()

    rows_flow.relay()
    rows_flow.complete()


def token_layer(
    act, cond, mask, vectors, rim, owner, atom_part, project_part, bias, ada, attn, out, tin, tout
):
    groups, ring = lax.axis_size("fsdp"), lax.axis_size("seq")
    rows, depth = act.shape
    width = ada.shape[1]
    dma = pltpu.SemaphoreType.DMA
    vmem, far = pl.BlockSpec(memory_space=pltpu.VMEM), pl.BlockSpec(memory_space=pl.ANY)
    half_type = jnp.bfloat16
    near = dict(
        act=act, cond=cond, mask=mask, vectors=vectors, rim=rim, owner=owner,
        atom_part=atom_part, project_part=project_part,
    )
    weights = dict(ada=ada, attn=attn, bias=bias, out=out, tin=tin, tout=tout)
    outs = dict(
        token=((rows, depth), half_type),
        rows_all=((ring, rows, project_part.shape[1]), half_type),
        rim_all=(rim.shape, rim.dtype),
        owner_all=(owner.shape, owner.dtype),
        atom_all=((groups,) + atom_part.shape, half_type),
    )
    packed = (groups, groups, rows // 2, 2 * width)
    chains = 4 + 2 * groups
    hops = max(groups - 1, 1)
    length = ring // 2
    scratch = {name: pltpu.VMEM(array.shape, array.dtype) for name, array in weights.items()}
    scratch |= dict(
        conds=pltpu.VMEM((groups, rows, depth), half_type),
        act_out=pltpu.VMEM(packed[1:], half_type),
        acts=pltpu.VMEM(packed[1:], half_type),
        attend=pltpu.VMEM(packed, half_type),
        transit=pltpu.VMEM(packed, half_type),
        queries=pltpu.VMEM((groups, rows, width), half_type),
        gates=pltpu.VMEM((groups, rows, width), half_type),
        gated=pltpu.VMEM((groups, rows, width), half_type),
        kv=pltpu.VMEM((ring, groups, rows, 2 * width), half_type),
        masks=pltpu.VMEM((ring, 1, rows), jnp.int32),
        project=pltpu.VMEM((groups,) + project_part.shape, half_type),
        total=pltpu.VMEM((groups, rows, depth), jnp.float32),
        sums_out=pltpu.VMEM((groups, rows, depth), half_type),
        sums_in=pltpu.VMEM((2, groups, rows, depth), half_type),
        load=dma((len(weights),)),
        line_send=dma((chains, 2, hops)),
        line_recv=dma((chains, 2, hops)),
        act_send=dma((groups,)),
        act_recv=dma((groups,)),
        seq_send=dma((groups + 2, 2, max(length - 1, 1))),
        seq_recv=dma((groups + 2, 2, max(length - 1, 1))),
        hand_send=dma((groups + 2, 2 * length)),
        hand_recv=dma((groups + 2, 2 * length)),
        halo_send=dma((2, 2)),
        halo_recv=dma((2, 2)),
        swap_send=dma((2,)),
        swap_recv=dma((2,)),
        sum_send=dma((2, groups, 2)),
        sum_recv=dma((2, groups, 2)),
    )
    names = list(near) + [name + "_hbm" for name in weights] + list(outs) + list(scratch)
    results = pl.pallas_call(
        functools.partial(token_kernel, tuple(names), groups, ring),
        out_shape=tuple(jax.ShapeDtypeStruct(*out) for out in outs.values()),
        in_specs=[vmem] * len(near) + [far] * len(weights),
        out_specs=tuple([vmem] * len(outs)),
        scratch_shapes=list(scratch.values()),
        compiler_params=pltpu.CompilerParams(
            collective_id=1, has_side_effects=True, vmem_limit_bytes=VMEM_LIMIT
        ),
        name="token_layer",
    )(*near.values(), *weights.values())
    return results


class Halo:
    def __init__(self, axis, size, block, out, send, recv):
        self.axis, self.size, self.block, self.out = axis, size, block, out
        self.send, self.recv = send, recv
        self.index = lax.axis_index(axis)
        self.above, self.below = self.index > 0, self.index < size - 1

    def greet(self, barrier):
        for present, target in ((self.above, self.index - 1), (self.below, self.index + 1)):

            @pl.when(present)
            def _():
                pl.semaphore_signal(
                    barrier, inc=1, device_id={self.axis: target}, device_id_type=MESH
                )

        return jnp.where(self.above, 1, 0) + jnp.where(self.below, 1, 0)

    def copy(self, side):
        return pltpu.make_async_remote_copy(
            src_ref=self.block.at[side],
            dst_ref=self.out.at[1 - side],
            send_sem=self.send.at[side],
            recv_sem=self.recv.at[side],
            device_id={self.axis: self.index - 1 + 2 * side},
            device_id_type=MESH,
        )

    def begin(self):
        for side, present in ((0, self.above), (1, self.below)):

            @pl.when(present)
            def _():
                self.copy(side).start()

            @pl.when(jnp.logical_not(present))
            def _():
                self.out[side] = jnp.zeros(self.out.shape[1:], self.out.dtype)

    def steps(self):
        return 0

    def finish(self):
        for side, present in ((0, self.above), (1, self.below)):

            @pl.when(present)
            def _():
                self.copy(side).wait_send()
                self.copy(1 - side).wait_recv()


def atom_kernel(
    first_ref, bounds_ref, rows_ref, skip_ref, cond_ref, rim_ref, token_ref, weight_ref, vector_ref,
    position_ref, bias_ref, out_ref, state_ref, query_ref, gate_ref, key_ref, value_ref, held_ref,
):
    count, channels = query_ref.shape
    head_width = channels // HA
    tokens = rows_ref.shape[0]
    chunk = min(512, tokens)
    inner = pl.ds(RIM, count)
    owners = token_ref[...]
    taken = jnp.zeros((owners.shape[0], channels), jnp.float32)
    for start in range(0, tokens, chunk):
        column = lax.broadcasted_iota(jnp.int32, (owners.shape[0], chunk), 1) + start
        hit = jnp.where(owners == column, 1.0, 0.0).astype(jnp.bfloat16)
        taken = taken + matmul(hit, rows_ref[start : start + chunk, :])
    skip = jnp.concatenate([rim_ref[0, :, :channels], skip_ref[...], rim_ref[1, :, :channels]], axis=0)
    cond = jnp.concatenate([rim_ref[0, :, channels:], cond_ref[...], rim_ref[1, :, channels:]], axis=0)
    state = skip.astype(jnp.float32) + taken
    state_ref[...] = state
    normed = layer_norm(cond).astype(jnp.bfloat16)
    atom_x = (
        jax.nn.sigmoid(matmul_t(normed, weight_ref[0]) + vector_ref[0:1, :]) * layer_norm(state)
        + matmul_t(normed, weight_ref[1])
    ).astype(jnp.bfloat16)
    own_x = atom_x[RIM : RIM + count, :]
    query_ref[...] = (matmul_t(own_x, weight_ref[2]) + vector_ref[1:2, :]).astype(jnp.bfloat16)
    gate_ref[...] = matmul_t(own_x, weight_ref[5]).astype(jnp.bfloat16)
    key_ref[...] = matmul_t(atom_x, weight_ref[3]).astype(jnp.bfloat16)
    value_ref[...] = matmul_t(atom_x, weight_ref[4]).astype(jnp.bfloat16)
    head_of = lax.broadcasted_iota(jnp.int32, (WQ, channels), 1) // head_width
    lane = lax.broadcasted_iota(jnp.int32, (1, WK), 1)
    scale = 1.0 / math.sqrt(head_width)

    def windows(step, carry):
        scores = []
        bases = [pl.multiple_of(step * (BATCH * WQ) + i * WQ, WQ) for i in range(BATCH)]
        for i, base in enumerate(bases):
            queries = query_ref[pl.ds(base, WQ), :]
            stacked = jnp.concatenate(
                [jnp.where(head_of == head, queries, 0).astype(jnp.bfloat16) for head in range(HA)],
                axis=0,
            )
            score = lax.dot_general(
                stacked, key_ref[pl.ds(base, WK), :], (((1,), (1,)), ((), ())),
                preferred_element_type=jnp.float32,
            )
            bias = bias_ref[:, pl.ds(base, WQ), :].reshape(HA * WQ, WK).astype(jnp.float32)
            slot = first_ref[0] + base - RIM + lane
            index = step * BATCH + i
            inside = (slot >= bounds_ref[2 * index]) & (slot < bounds_ref[2 * index + 1])
            scores.append(jnp.where(inside, score * scale + bias, FAR))
        weights = [jnp.exp(score - jnp.max(score, axis=-1, keepdims=True)) for score in scores]
        results = []
        for base, weight in zip(bases, weights):
            attended = matmul(weight.astype(jnp.bfloat16), value_ref[pl.ds(base, WK), :])
            attended = attended / jnp.sum(weight, axis=-1, keepdims=True)
            result = jnp.zeros((WQ, channels), jnp.float32)
            for head in range(HA):
                result = result + jnp.where(
                    head_of == head, attended[head * WQ : (head + 1) * WQ], 0.0
                )
            results.append(result)
        start = pl.multiple_of(step * (BATCH * WQ), BATCH * WQ)
        held_ref[pl.ds(start, BATCH * WQ), :] = jnp.concatenate(results, axis=0)
        return carry

    lax.fori_loop(0, count // (BATCH * WQ), windows, 0)
    gated = (held_ref[...] * jax.nn.sigmoid(gate_ref[...].astype(jnp.float32))).astype(jnp.bfloat16)
    fresh = state_ref[inner, :] + matmul_t(gated, weight_ref[6])
    final = layer_norm(fresh).astype(jnp.bfloat16)
    moved = matmul_t(position_ref[...], final)
    for axis in range(out_ref.shape[0]):
        out_ref[axis] = moved[axis : axis + 1, :]


BATCH = 8


def atom_block(first, bounds, rows, skip, cond, rims, owners, weights, vectors, positions, bias):
    count, channels = bias.shape[1], skip.shape[1]
    extended = skip.shape[0] + 2 * RIM
    smem = pl.BlockSpec(memory_space=pltpu.SMEM)
    vmem = pl.BlockSpec(memory_space=pltpu.VMEM)
    return pl.pallas_call(
        atom_kernel,
        in_specs=[smem, smem] + [vmem] * 9,
        out_specs=vmem,
        out_shape=jax.ShapeDtypeStruct((positions.shape[0], 1, count), jnp.float32),
        scratch_shapes=[
            pltpu.VMEM((extended, channels), jnp.float32),
            pltpu.VMEM((count, channels), jnp.bfloat16),
            pltpu.VMEM((count, channels), jnp.bfloat16),
            pltpu.VMEM((extended, channels), jnp.bfloat16),
            pltpu.VMEM((extended, channels), jnp.bfloat16),
            pltpu.VMEM((count, channels), jnp.float32),
        ],
        compiler_params=pltpu.CompilerParams(vmem_limit_bytes=VMEM_LIMIT),
        name="atom_block",
    )(first, bounds, rows, skip, cond, rims, owners, weights, vectors, positions, bias)


def rims(array):
    return jnp.stack([array[:RIM], array[array.shape[0] - RIM :]])


def per_device(
    token_act,
    token_cond,
    pair_bias,
    token_mask,
    ada_weights,
    attention_in,
    attention_out,
    transition_in,
    transition_out,
    token_vectors,
    atom_skip,
    atom_cond,
    atom_bias,
    window_bounds,
    atom_token,
    atom_weights,
    token_to_atom,
    atom_vectors,
    position_out,
):
    groups = lax.axis_size("fsdp")
    width = attention_in.shape[2]
    channels = atom_cond.shape[1]
    atom_rims = rims(jnp.concatenate([atom_skip[0], atom_cond], axis=1))
    owner_rims = jnp.pad(rims(atom_token)[:, None, :], ((0, 0), (0, 0), (0, 2 * WK - RIM)))
    vectors = jnp.transpose(token_vectors.reshape(-1, groups, width), (1, 0, 2))
    token_result, all_rows, atom_rims, owner_rims, atom_all = token_layer(
        token_act[0],
        token_cond[0],
        token_mask[None],
        vectors,
        atom_rims,
        owner_rims,
        jnp.swapaxes(atom_weights, 1, 2).reshape(-1, channels),
        token_to_atom,
        pair_bias,
        jnp.swapaxes(ada_weights, 1, 2),
        jnp.swapaxes(attention_in, 1, 2),
        attention_out,
        transition_in,
        transition_out,
    )
    owners = jnp.concatenate([owner_rims[0, 0, :RIM], atom_token, owner_rims[1, 0, :RIM]])[:, None]
    count = atom_weights.shape[0]
    atom_full = jnp.transpose(
        atom_all.reshape(groups, count, -1, channels), (1, 0, 2, 3)
    ).reshape(count, channels, channels)
    first_atom = (lax.axis_index("seq") * atom_cond.shape[0]).astype(jnp.int32).reshape(1)
    update = atom_block(
        first_atom,
        window_bounds.reshape(-1),
        all_rows.reshape(-1, channels),
        atom_skip[0],
        atom_cond,
        atom_rims,
        owners,
        atom_full,
        atom_vectors,
        position_out,
        atom_bias,
    )
    return (token_result[None], jnp.transpose(update, (1, 0, 2)))


def solution(mesh):
    in_specs = (
        P(("sample", "fsdp"), "seq", None),
        P(("sample", "fsdp"), "seq", None),
        P("fsdp", "seq", None),
        P("seq"),
        P(None, None, "fsdp"),
        P(None, None, "fsdp"),
        P("fsdp", None),
        P(None, None, "fsdp"),
        P("fsdp", None),
        P(),
        P(("sample", "fsdp"), "seq", None),
        P("seq", None),
        P(None, "seq", None),
        P("seq", None),
        P("seq"),
        P(None, None, "fsdp"),
        P("fsdp", None),
        P(),
        P(),
    )
    out_specs = (P(("sample", "fsdp"), "seq", None), P(("sample", "fsdp"), None, "seq"))
    return jax.shard_map(
        per_device, mesh=mesh, in_specs=in_specs, out_specs=out_specs, check_vma=False
    )
```

time: 148 us -> 97.1 us (0.66); the launches traced: 145 us -> 96.6 us
  Pallas kernels: 103 us -> 86.2 us
  matrix products: 14.7 us -> 0 us
  local copies, waits for them, and re-layouts: 17.1 us -> 8.41 us
  other arithmetic: 9.65 us -> 1.4 us
    pallas_call x5 -> x1, Pallas kernels: 96 us -> 79.6 us  [token_layer(): pl.pallas_call(functools.partial(token_kernel, tuple(names), groups, ring...]
    dot_general x11 -> x0, matrix products: 14.7 us -> none  [matmul(): return jnp.dot(left_side, right_side, preferred_element_type=jnp.float32)]
    concatenate x6 -> x0, other arithmetic: 4.1 us -> none  [the longest x3 2.35 us: pack(): jnp.concatenate([array[..., :half, :], array[..., half:, :]], axis=-1)]
    slice x9 -> x0, local copies, waits for them, and re-layouts: 3.61 us -> none  [the longest x3 2.84 us: unpack(): return jnp.concatenate([array[..., :half], array[..., half:]], axis=-2)]
    unnamed x45 -> x6, local copies, waits for them, and re-layouts: 4.69 us -> 1.44 us
    reduce_sum x4 -> x0, other arithmetic: 2.55 us -> none  [the longest x2 1.32 us: layer_norm(): spread = jnp.mean(center * center, axis=-1, keepdims=True)]
    convert_element_type x8 -> x0, local copies, waits for them, and re-layouts: 2.53 us -> none  [the longest x4 1.94 us: grouped(): return array.astype(jnp.bfloat16).reshape(groups, row_count, -1)]
    transpose x4 -> x0, local copies, waits for them, and re-layouts: 2.33 us -> none  [the longest x2 1.96 us: joined(): return jnp.transpose(array, (1, 2, 0, 3)).reshape(groups * row_count, depth)]
where the time goes in v1:
time: 97.1 us; the launch traced here: 96.6 us
  Pallas kernels  86.2 us (89%)
  local copies, waits for them, and re-layouts  8.41 us (9%)
  other arithmetic  1.4 us (1%)
    pallas_call x1, Pallas kernels, token_layer(): pl.pallas_call(functools.partial(token_kernel, tuple(names), groups, ring...  79.6 us
    pallas_call x1, Pallas kernels, atom_block(): pl.pallas_call(atom_kernel, in_specs=[smem, smem] + [vmem] * 9, out_specs...  6.58 us

profile of v1, /device:TPU:0, one launch (start us, length us, event | category | flops | bytes accessed | tf_op | source)
XLA Modules:
  0.0 96.6 jit_solution(8015403722710445373)
XLA Ops:
  0.6 0.8 slice_bitcast_fusion.3
  1.5 0.6 pad.4.refs_5_
  2.1 0.8 reshape.25
  2.9 0.6 copy.30
  3.5 0.8 copy.26
  4.2 0.7 reshape.28.bounds_ref
  4.9 0.8 maximum_bitcast_fusion
  5.7 0.6 pad_maximum_fusion.refs_4_
  6.3 0.0 copy-start.1
  6.3 79.6 %token_layer.1 = (bf16[128,768]{1,0:T(8,128)(2,1)}, bf16[4,128,128]{2,1,0:T(8,128)(2,1)}, bf16[2,48,256]{2,1,0:T(8,128)(2,1)}, s32[2,1,256]{2,1,0:T(1,128)}, bf16[4,224,128]{2,1,0:T(8,128)(2,1)}) custom-call(bf16[128,768]{1,0:T(8,128)(2,1)} %bitcast.42, bf16[128,768]{1,0:T(8,128)(2,1)} %bitcast.43, s32[1,128]{1,0:T(1,128)} %bitcast.49, ...), custom_call_target="tpu_custom_call" | custom-call | tf_op jit(solution)/shard_map/token_layer/pallas_call | solution.py:527
  85.9 0.7 slice_bitcast_fusion
  86.6 0.0 copy-done.1
  86.6 0.1 concatenate.7
  86.7 1.7 %copy.27 = bf16[4,7,32,128]{3,2,0,1:T(8,128)(2,1)} copy(bf16[4,7,32,128]{3,2,1,0:T(8,128)(2,1)} %bitcast.40) | data formatting | bytes 458752 | tf_op jit(solution)/shard_map/reshape | solution.py:743
  88.3 1.0 %broadcast_in_dim.16.token_ref = s32[1120,1]{1,0:T(8,128)} reshape(s32[1120]{0:T(1024)S(1)} %concatenate.7) | data formatting | bytes 8960 | tf_op jit(solution)/shard_map/broadcast_in_dim | solution.py:740
  89.4 0.0 copy-start
  89.4 6.6 %atom_block.1 = f32[3,1,1024]{2,1,0:T(1,128)} custom-call(s32[1]{0:T(128)} %bitcast.16.first_ref, s32[64]{0:T(128)} %reshape.28.bounds_ref, bf16[512,128]{1,0:T(8,128)(2,1)} %bitcast.44, bf16[1024,128]{1,0:T(8,128)(2,1)} %bitcast.38, bf16[1024,128]{1,0:T(8,128)(2,1)} %cond_ref.1, bf16[2,48,256]{2,1,0:T(8,128)(2,1)} %get-tuple-element.9.rim_ref, ...), custom_call_target="tpu_custom_call" | custom-call | tf_op jit(solution)/shard_map/atom_block/pallas_call | solution.py:675
  96.0 0.0 copy-done
  96.0 0.7 copy.32
  (1 shorter events, 0.0 us)
Async XLA Ops:
  6.3 80.3 %copy-start.1 = (s32[1024]{0:T(1024)S(1)}, s32[1024]{0:T(1024)}, u32[]{:S(2)}) copy-start(s32[1024]{0:T(1024)} %param.33) | copy-start | bytes 12292
  89.4 6.6 %copy-start = (bf16[128,768]{1,0:T(8,128)(2,1)S(1)}, bf16[128,768]{1,0:T(8,128)(2,1)}, u32[]{:S(2)}) copy-start(bf16[128,768]{1,0:T(8,128)(2,1)} %get-tuple-element.7) | copy-start | bytes 589828

commit v2 on v1

--- a/solution.py
+++ b/solution.py
@@ -16,6 +16,8 @@
 EPS = 1e-05
 FAR = -1e30
 RIM = (WK - WQ) // 2
+ATOM_MAPS = 7
+BATCH = 8
 VMEM_LIMIT = 56 * 1024 * 1024
 MESH = pl.DeviceIdType.MESH
 
@@ -201,6 +203,50 @@
                     self.hand(self.key(side, step), self.origin(side, step), True).wait_recv()
 
 
+class Halo:
+    def __init__(self, axis, size, pieces, homes, send, recv, number):
+        self.axis, self.pieces, self.homes = axis, pieces, homes
+        self.send, self.recv, self.number = send, recv, number
+        self.index = lax.axis_index(axis)
+        self.present = self.index > 0, self.index < size - 1
+
+    def greet(self, signal):
+        for side in (0, 1):
+
+            @pl.when(self.present[side])
+            def _():
+                signal(self.axis, self.index - 1 + 2 * side)
+
+        return jnp.where(self.present[0], 1, 0) + jnp.where(self.present[1], 1, 0)
+
+    def copy(self, side):
+        at = (self.number, side)
+        return remote(
+            self.pieces[side], self.homes[1 - side], self.send.at[at], self.recv.at[at],
+            self.axis, self.index - 1 + 2 * side,
+        )
+
+    def begin(self):
+        for side in (0, 1):
+            home = self.homes[side]
+
+            @pl.when(self.present[side])
+            def _():
+                self.copy(side).start()
+
+            @pl.when(jnp.logical_not(self.present[side]))
+            def _():
+                home[...] = jnp.zeros(home.shape, home.dtype)
+
+    def finish(self):
+        for side in (0, 1):
+
+            @pl.when(self.present[side])
+            def _():
+                self.copy(side).wait_send()
+                self.copy(1 - side).wait_recv()
+
+
 def token_kernel(names, groups, ring, *refs):
     r = types.SimpleNamespace(**dict(zip(names, refs)))
     me, seat = lax.axis_index("fsdp"), lax.axis_index("seq")
@@ -216,15 +262,30 @@
 
     loads = {
         name: pltpu.make_async_copy(getattr(r, name + "_hbm"), getattr(r, name), r.load.at[number])
-        for number, name in enumerate(("ada", "attn", "bias", "out", "tin", "tout"))
+        for number, name in enumerate(("ada", "attn", "bias", "out", "tin", "tout", "atom_bias"))
     }
+    count, channels = r.skip_hbm.shape
+    inner_atoms = pl.ds(RIM, count)
+    for number, name in enumerate(("skip", "atom_cond")):
+        loads[name] = pltpu.make_async_copy(
+            getattr(r, name + "_hbm"), getattr(r, name).at[inner_atoms], r.load.at[len(loads)]
+        )
 
     def pairs(view, *prefix):
         return Pairs("seq", ring, view, r.seq_send, r.seq_recv, r.hand_send, r.hand_recv, prefix)
 
     halos = [
-        Halo("seq", ring, r.rim, r.rim_all, r.halo_send.at[0], r.halo_recv.at[0]),
-        Halo("seq", ring, r.owner, r.owner_all, r.halo_send.at[1], r.halo_recv.at[1]),
+        Halo(
+            "seq", ring, [source.at[pl.ds(start, RIM)] for start in (0, count - RIM)],
+            [home.at[pl.ds(start, RIM)] for start in (0, RIM + count)], r.halo_send, r.halo_recv, number,
+        )
+        for number, (source, home) in enumerate(((r.skip_hbm, r.skip), (r.atom_cond_hbm, r.atom_cond)))
+    ]
+    halos += [
+        Halo(
+            "seq", ring, [r.owner_ends.at[0], r.owner_ends.at[r.owner_ends.shape[0] - 1]],
+            [r.owner_rims.at[0], r.owner_rims.at[1]], r.halo_send, r.halo_recv, 2,
+        )
     ]
     kv_flows = [pairs(lambda slot, g=g: r.kv.at[slot, g], g) for g in range(groups)]
     mask_flow = pairs(lambda slot: r.masks.at[slot], groups)
@@ -232,7 +293,7 @@
 
     for shift in range(1, groups):
         signal("fsdp", lax.rem(me + shift, groups))
-    expected = last + mask_flow.greet(signal) + halos[0].greet(barrier)
+    expected = last + mask_flow.greet(signal) + halos[0].greet(signal)
     for load in loads.values():
         load.start()
 
@@ -420,6 +481,92 @@
                         r.sums_out[g, piece] = r.total[g, piece].astype(jnp.bfloat16)
                         hop(side, g, part).start()
 
+    heads_out = lax.broadcasted_iota(jnp.int32, (WQ, channels), 1) // (channels // HA)
+    tokens = ring * rows
+
+    def atom_weight(i):
+        high = r.atom_part.shape[0] // ATOM_MAPS
+        return r.atom_all[:, i * high : (i + 1) * high, :].reshape(channels, channels)
+
+    def atom_before():
+        normed = layer_norm(r.atom_cond[...]).astype(jnp.bfloat16)
+        r.atom_gain[...] = jax.nn.sigmoid(matmul_t(normed, atom_weight(0)) + r.atom_vectors[0:1, :])
+        r.atom_shift[...] = matmul_t(normed, atom_weight(1))
+        blocks = r.owner.shape[0]
+
+        def hit(column, start):
+            span = min(512, tokens)
+            for first in range(0, tokens, span):
+                token = lax.broadcasted_iota(jnp.int32, (column.shape[0], span), 1) + first
+                found = jnp.where(column == token.astype(jnp.float32), 1.0, 0.0).astype(jnp.bfloat16)
+                r.hits[pl.ds(start, column.shape[0]), pl.ds(first, span)] = found
+
+        owners = jnp.transpose(r.owner[...].astype(jnp.float32))
+        for block in range(blocks):
+            hit(owners[:, block : block + 1], RIM + block * WK)
+        for side, home in ((0, 0), (1, RIM + count)):
+            ends = jnp.broadcast_to(r.owner_rims[side].astype(jnp.float32), (8, WK))
+            column = jnp.transpose(ends)[:, 0:1]
+            hit(column[WK - RIM :] if side == 0 else column[:RIM], home)
+        lane = lax.broadcasted_iota(jnp.int32, (1, WK), 1)
+
+        def window(index, carry):
+            base = pl.multiple_of(index * WQ, WQ)
+            slot = seat * count + base - RIM + lane
+            inside = (slot >= r.bounds[0, index]) & (slot < r.bounds[1, index])
+            bias = r.atom_bias[:, pl.ds(base, WQ), :].reshape(HA * WQ, WK).astype(jnp.float32)
+            r.masked[index] = jnp.where(inside, bias, FAR)
+            return carry
+
+        lax.fori_loop(0, count // WQ, window, 0)
+
+    def atom_after():
+        taken = matmul(r.hits[...], r.rows_all[...].reshape(tokens, channels))
+        state = r.skip[...].astype(jnp.float32) + taken
+        r.state[...] = state[RIM : RIM + count]
+        atom_x = (r.atom_gain[...] * layer_norm(state) + r.atom_shift[...]).astype(jnp.bfloat16)
+        own_x = atom_x[RIM : RIM + count, :]
+        r.atom_query[...] = (matmul_t(own_x, atom_weight(2)) + r.atom_vectors[1:2, :]).astype(jnp.bfloat16)
+        r.atom_key[...] = matmul_t(atom_x, atom_weight(3)).astype(jnp.bfloat16)
+        r.atom_value[...] = matmul_t(atom_x, atom_weight(4)).astype(jnp.bfloat16)
+        r.atom_gate[...] = jax.nn.sigmoid(matmul_t(own_x, atom_weight(5)).astype(jnp.bfloat16).astype(jnp.float32))
+        scale = 1.0 / math.sqrt(channels // HA)
+
+        def windows(step, carry):
+            bases = [pl.multiple_of(step * (BATCH * WQ) + i * WQ, WQ) for i in range(BATCH)]
+            scores = []
+            for i, base in enumerate(bases):
+                queries = r.atom_query[pl.ds(base, WQ), :]
+                stacked = jnp.concatenate(
+                    [jnp.where(heads_out == head, queries, 0).astype(jnp.bfloat16) for head in range(HA)],
+                    axis=0,
+                )
+                score = matmul_t(stacked, r.atom_key[pl.ds(base, WK), :])
+                masked = r.masked[step * BATCH + i]
+                scores.append(jnp.where(masked > 0.5 * FAR, score * scale + masked, FAR))
+            weights = [jnp.exp(score - jnp.max(score, axis=-1, keepdims=True)) for score in scores]
+            results = []
+            for base, weight in zip(bases, weights):
+                attended = matmul(weight.astype(jnp.bfloat16), r.atom_value[pl.ds(base, WK), :])
+                attended = attended / jnp.sum(weight, axis=-1, keepdims=True)
+                result = jnp.zeros((WQ, channels), jnp.float32)
+                for head in range(HA):
+                    result = result + jnp.where(
+                        heads_out == head, attended[head * WQ : (head + 1) * WQ], 0.0
+                    )
+                results.append(result)
+            start = pl.multiple_of(step * (BATCH * WQ), BATCH * WQ)
+            r.held[pl.ds(start, BATCH * WQ), :] = jnp.concatenate(results, axis=0)
+            return carry
+
+        lax.fori_loop(0, count // (BATCH * WQ), windows, 0)
+        gated = (r.held[...] * r.atom_gate[...]).astype(jnp.bfloat16)
+        fresh = r.state[...] + matmul_t(gated, atom_weight(6))
+        final = layer_norm(fresh).astype(jnp.bfloat16)
+        moved = matmul_t(r.position[...], final)
+        for axis in range(moved.shape[0]):
+            r.update[axis] = moved[axis : axis + 1, :]
+
     for name in ("out", "tin", "tout"):
         loads[name].wait()
     for g in outer:
@@ -432,11 +579,19 @@
         flow.arrive(last - 1)
     for copy in swaps():
         copy.start()
+    for name in ("skip", "atom_cond", "atom_bias"):
+        loads[name].wait()
+    for halo in halos:
+        halo.finish()
+    for copy in swaps():
+        copy.wait()
     for stage in range(1, last):
         for g in outer:
             reduce(stage, g)
-    for copy in swaps():
-        copy.wait()
+        if stage == 1:
+            atom_before()
+    if last == 1:
+        atom_before()
     for side, present in ((0, me > 0), (1, me < last)):
 
         @pl.when(present)
@@ -452,8 +607,6 @@
         flow.drain()
     for shift in range(1, groups):
         slots(shift, False).wait_send()
-    for halo in halos:
-        halo.finish()
     for g in range(groups):
         for side, goes in ((0, g > me), (1, g < me)):
 
@@ -464,35 +617,45 @@
 
     rows_flow.relay()
     rows_flow.complete()
-
-
-def token_layer(
-    act, cond, mask, vectors, rim, owner, atom_part, project_part, bias, ada, attn, out, tin, tout
-):
+    atom_after()
+
+
+def token_layer(near, weights, bounds):
     groups, ring = lax.axis_size("fsdp"), lax.axis_size("seq")
-    rows, depth = act.shape
-    width = ada.shape[1]
+    rows, depth = near["act"].shape
+    width = weights["ada"].shape[1]
+    count, channels = weights["skip"].shape
+    extended = count + 2 * RIM
     dma = pltpu.SemaphoreType.DMA
     vmem, far = pl.BlockSpec(memory_space=pltpu.VMEM), pl.BlockSpec(memory_space=pl.ANY)
     half_type = jnp.bfloat16
-    near = dict(
-        act=act, cond=cond, mask=mask, vectors=vectors, rim=rim, owner=owner,
-        atom_part=atom_part, project_part=project_part,
-    )
-    weights = dict(ada=ada, attn=attn, bias=bias, out=out, tin=tin, tout=tout)
+    project_part, atom_part = near["project_part"], near["atom_part"]
     outs = dict(
         token=((rows, depth), half_type),
-        rows_all=((ring, rows, project_part.shape[1]), half_type),
-        rim_all=(rim.shape, rim.dtype),
-        owner_all=(owner.shape, owner.dtype),
-        atom_all=((groups,) + atom_part.shape, half_type),
+        update=((near["position"].shape[0], 1, count), jnp.float32),
     )
     packed = (groups, groups, rows // 2, 2 * width)
     chains = 4 + 2 * groups
     hops = max(groups - 1, 1)
     length = ring // 2
     scratch = {name: pltpu.VMEM(array.shape, array.dtype) for name, array in weights.items()}
+    atoms = lambda height, kind: pltpu.VMEM((height, channels), kind)
     scratch |= dict(
+        skip=atoms(extended, half_type),
+        atom_cond=atoms(extended, half_type),
+        atom_gain=atoms(extended, jnp.float32),
+        atom_shift=atoms(extended, jnp.float32),
+        atom_key=atoms(extended, half_type),
+        atom_value=atoms(extended, half_type),
+        atom_query=atoms(count, half_type),
+        atom_gate=atoms(count, jnp.float32),
+        state=atoms(count, jnp.float32),
+        held=atoms(count, jnp.float32),
+        hits=pltpu.VMEM((extended, ring * rows), half_type),
+        masked=pltpu.VMEM((count // WQ, HA * WQ, WK), jnp.float32),
+        owner_rims=pltpu.VMEM((2, 1, near["owner"].shape[1]), jnp.int32),
+        rows_all=pltpu.VMEM((ring, rows, channels), half_type),
+        atom_all=pltpu.VMEM((groups,) + atom_part.shape, half_type),
         conds=pltpu.VMEM((groups, rows, depth), half_type),
         act_out=pltpu.VMEM(packed[1:], half_type),
         acts=pltpu.VMEM(packed[1:], half_type),
@@ -516,182 +679,25 @@
         seq_recv=dma((groups + 2, 2, max(length - 1, 1))),
         hand_send=dma((groups + 2, 2 * length)),
         hand_recv=dma((groups + 2, 2 * length)),
-        halo_send=dma((2, 2)),
-        halo_recv=dma((2, 2)),
+        halo_send=dma((3, 2)),
+        halo_recv=dma((3, 2)),
         swap_send=dma((2,)),
         swap_recv=dma((2,)),
         sum_send=dma((2, groups, 2)),
         sum_recv=dma((2, groups, 2)),
     )
-    names = list(near) + [name + "_hbm" for name in weights] + list(outs) + list(scratch)
-    results = pl.pallas_call(
+    names = ["bounds"] + list(near) + [name + "_hbm" for name in weights] + list(outs) + list(scratch)
+    return pl.pallas_call(
         functools.partial(token_kernel, tuple(names), groups, ring),
         out_shape=tuple(jax.ShapeDtypeStruct(*out) for out in outs.values()),
-        in_specs=[vmem] * len(near) + [far] * len(weights),
+        in_specs=[pl.BlockSpec(memory_space=pltpu.SMEM)] + [vmem] * len(near) + [far] * len(weights),
         out_specs=tuple([vmem] * len(outs)),
         scratch_shapes=list(scratch.values()),
         compiler_params=pltpu.CompilerParams(
             collective_id=1, has_side_effects=True, vmem_limit_bytes=VMEM_LIMIT
         ),
         name="token_layer",
-    )(*near.values(), *weights.values())
-    return results
-
-
-class Halo:
-    def __init__(self, axis, size, block, out, send, recv):
-        self.axis, self.size, self.block, self.out = axis, size, block, out
-        self.send, self.recv = send, recv
-        self.index = lax.axis_index(axis)
-        self.above, self.below = self.index > 0, self.index < size - 1
-
-    def greet(self, barrier):
-        for present, target in ((self.above, self.index - 1), (self.below, self.index + 1)):
-
-            @pl.when(present)
-            def _():
-                pl.semaphore_signal(
-                    barrier, inc=1, device_id={self.axis: target}, device_id_type=MESH
-                )
-
-        return jnp.where(self.above, 1, 0) + jnp.where(self.below, 1, 0)
-
-    def copy(self, side):
-        return pltpu.make_async_remote_copy(
-            src_ref=self.block.at[side],
-            dst_ref=self.out.at[1 - side],
-            send_sem=self.send.at[side],
-            recv_sem=self.recv.at[side],
-            device_id={self.axis: self.index - 1 + 2 * side},
-            device_id_type=MESH,
-        )
-
-    def begin(self):
-        for side, present in ((0, self.above), (1, self.below)):
-
-            @pl.when(present)
-            def _():
-                self.copy(side).start()
-
-            @pl.when(jnp.logical_not(present))
-            def _():
-                self.out[side] = jnp.zeros(self.out.shape[1:], self.out.dtype)
-
-    def steps(self):
-        return 0
-
-    def finish(self):
-        for side, present in ((0, self.above), (1, self.below)):
-
-            @pl.when(present)
-            def _():
-                self.copy(side).wait_send()
-                self.copy(1 - side).wait_recv()
-
-
-def atom_kernel(
-    first_ref, bounds_ref, rows_ref, skip_ref, cond_ref, rim_ref, token_ref, weight_ref, vector_ref,
-    position_ref, bias_ref, out_ref, state_ref, query_ref, gate_ref, key_ref, value_ref, held_ref,
-):
-    count, channels = query_ref.shape
-    head_width = channels // HA
-    tokens = rows_ref.shape[0]
-    chunk = min(512, tokens)
-    inner = pl.ds(RIM, count)
-    owners = token_ref[...]
-    taken = jnp.zeros((owners.shape[0], channels), jnp.float32)
-    for start in range(0, tokens, chunk):
-        column = lax.broadcasted_iota(jnp.int32, (owners.shape[0], chunk), 1) + start
-        hit = jnp.where(owners == column, 1.0, 0.0).astype(jnp.bfloat16)
-        taken = taken + matmul(hit, rows_ref[start : start + chunk, :])
-    skip = jnp.concatenate([rim_ref[0, :, :channels], skip_ref[...], rim_ref[1, :, :channels]], axis=0)
-    cond = jnp.concatenate([rim_ref[0, :, channels:], cond_ref[...], rim_ref[1, :, channels:]], axis=0)
-    state = skip.astype(jnp.float32) + taken
-    state_ref[...] = state
-    normed = layer_norm(cond).astype(jnp.bfloat16)
-    atom_x = (
-        jax.nn.sigmoid(matmul_t(normed, weight_ref[0]) + vector_ref[0:1, :]) * layer_norm(state)
-        + matmul_t(normed, weight_ref[1])
-    ).astype(jnp.bfloat16)
-    own_x = atom_x[RIM : RIM + count, :]
-    query_ref[...] = (matmul_t(own_x, weight_ref[2]) + vector_ref[1:2, :]).astype(jnp.bfloat16)
-    gate_ref[...] = matmul_t(own_x, weight_ref[5]).astype(jnp.bfloat16)
-    key_ref[...] = matmul_t(atom_x, weight_ref[3]).astype(jnp.bfloat16)
-    value_ref[...] = matmul_t(atom_x, weight_ref[4]).astype(jnp.bfloat16)
-    head_of = lax.broadcasted_iota(jnp.int32, (WQ, channels), 1) // head_width
-    lane = lax.broadcasted_iota(jnp.int32, (1, WK), 1)
-    scale = 1.0 / math.sqrt(head_width)
-
-    def windows(step, carry):
-        scores = []
-        bases = [pl.multiple_of(step * (BATCH * WQ) + i * WQ, WQ) for i in range(BATCH)]
-        for i, base in enumerate(bases):
-            queries = query_ref[pl.ds(base, WQ), :]
-            stacked = jnp.concatenate(
-                [jnp.where(head_of == head, queries, 0).astype(jnp.bfloat16) for head in range(HA)],
-                axis=0,
-            )
-            score = lax.dot_general(
-                stacked, key_ref[pl.ds(base, WK), :], (((1,), (1,)), ((), ())),
-                preferred_element_type=jnp.float32,
-            )
-            bias = bias_ref[:, pl.ds(base, WQ), :].reshape(HA * WQ, WK).astype(jnp.float32)
-            slot = first_ref[0] + base - RIM + lane
-            index = step * BATCH + i
-            inside = (slot >= bounds_ref[2 * index]) & (slot < bounds_ref[2 * index + 1])
-            scores.append(jnp.where(inside, score * scale + bias, FAR))
-        weights = [jnp.exp(score - jnp.max(score, axis=-1, keepdims=True)) for score in scores]
-        results = []
-        for base, weight in zip(bases, weights):
-            attended = matmul(weight.astype(jnp.bfloat16), value_ref[pl.ds(base, WK), :])
-            attended = attended / jnp.sum(weight, axis=-1, keepdims=True)
-            result = jnp.zeros((WQ, channels), jnp.float32)
-            for head in range(HA):
-                result = result + jnp.where(
-                    head_of == head, attended[head * WQ : (head + 1) * WQ], 0.0
-                )
-            results.append(result)
-        start = pl.multiple_of(step * (BATCH * WQ), BATCH * WQ)
-        held_ref[pl.ds(start, BATCH * WQ), :] = jnp.concatenate(results, axis=0)
-        return carry
-
-    lax.fori_loop(0, count // (BATCH * WQ), windows, 0)
-    gated = (held_ref[...] * jax.nn.sigmoid(gate_ref[...].astype(jnp.float32))).astype(jnp.bfloat16)
-    fresh = state_ref[inner, :] + matmul_t(gated, weight_ref[6])
-    final = layer_norm(fresh).astype(jnp.bfloat16)
-    moved = matmul_t(position_ref[...], final)
-    for axis in range(out_ref.shape[0]):
-        out_ref[axis] = moved[axis : axis + 1, :]
-
-
-BATCH = 8
-
-
-def atom_block(first, bounds, rows, skip, cond, rims, owners, weights, vectors, positions, bias):
-    count, channels = bias.shape[1], skip.shape[1]
-    extended = skip.shape[0] + 2 * RIM
-    smem = pl.BlockSpec(memory_space=pltpu.SMEM)
-    vmem = pl.BlockSpec(memory_space=pltpu.VMEM)
-    return pl.pallas_call(
-        atom_kernel,
-        in_specs=[smem, smem] + [vmem] * 9,
-        out_specs=vmem,
-        out_shape=jax.ShapeDtypeStruct((positions.shape[0], 1, count), jnp.float32),
-        scratch_shapes=[
-            pltpu.VMEM((extended, channels), jnp.float32),
-            pltpu.VMEM((count, channels), jnp.bfloat16),
-            pltpu.VMEM((count, channels), jnp.bfloat16),
-            pltpu.VMEM((extended, channels), jnp.bfloat16),
-            pltpu.VMEM((extended, channels), jnp.bfloat16),
-            pltpu.VMEM((count, channels), jnp.float32),
-        ],
-        compiler_params=pltpu.CompilerParams(vmem_limit_bytes=VMEM_LIMIT),
-        name="atom_block",
-    )(first, bounds, rows, skip, cond, rims, owners, weights, vectors, positions, bias)
-
-
-def rims(array):
-    return jnp.stack([array[:RIM], array[array.shape[0] - RIM :]])
+    )(bounds, *near.values(), *weights.values())
 
 
 def per_device(
@@ -718,44 +724,30 @@
     groups = lax.axis_size("fsdp")
     width = attention_in.shape[2]
     channels = atom_cond.shape[1]
-    atom_rims = rims(jnp.concatenate([atom_skip[0], atom_cond], axis=1))
-    owner_rims = jnp.pad(rims(atom_token)[:, None, :], ((0, 0), (0, 0), (0, 2 * WK - RIM)))
-    vectors = jnp.transpose(token_vectors.reshape(-1, groups, width), (1, 0, 2))
-    token_result, all_rows, atom_rims, owner_rims, atom_all = token_layer(
-        token_act[0],
-        token_cond[0],
-        token_mask[None],
-        vectors,
-        atom_rims,
-        owner_rims,
-        jnp.swapaxes(atom_weights, 1, 2).reshape(-1, channels),
-        token_to_atom,
-        pair_bias,
-        jnp.swapaxes(ada_weights, 1, 2),
-        jnp.swapaxes(attention_in, 1, 2),
-        attention_out,
-        transition_in,
-        transition_out,
+    near = dict(
+        act=token_act[0],
+        cond=token_cond[0],
+        mask=token_mask[None],
+        vectors=jnp.transpose(token_vectors.reshape(-1, groups, width), (1, 0, 2)),
+        owner=atom_token.reshape(-1, WK),
+        owner_ends=atom_token.reshape(-1, 1, WK),
+        atom_part=jnp.swapaxes(atom_weights, 1, 2).reshape(-1, channels),
+        project_part=token_to_atom,
+        atom_vectors=atom_vectors,
+        position=position_out,
     )
-    owners = jnp.concatenate([owner_rims[0, 0, :RIM], atom_token, owner_rims[1, 0, :RIM]])[:, None]
-    count = atom_weights.shape[0]
-    atom_full = jnp.transpose(
-        atom_all.reshape(groups, count, -1, channels), (1, 0, 2, 3)
-    ).reshape(count, channels, channels)
-    first_atom = (lax.axis_index("seq") * atom_cond.shape[0]).astype(jnp.int32).reshape(1)
-    update = atom_block(
-        first_atom,
-        window_bounds.reshape(-1),
-        all_rows.reshape(-1, channels),
-        atom_skip[0],
-        atom_cond,
-        atom_rims,
-        owners,
-        atom_full,
-        atom_vectors,
-        position_out,
-        atom_bias,
+    weights = dict(
+        ada=jnp.swapaxes(ada_weights, 1, 2),
+        attn=jnp.swapaxes(attention_in, 1, 2),
+        bias=pair_bias,
+        out=attention_out,
+        tin=transition_in,
+        tout=transition_out,
+        atom_bias=atom_bias,
+        skip=atom_skip[0],
+        atom_cond=atom_cond,
     )
+    token_result, update = token_layer(near, weights, jnp.swapaxes(window_bounds, 0, 1))
     return (token_result[None], jnp.transpose(update, (1, 0, 2)))
 
 

time: 97.1 us -> 89.8 us (0.925)
  local copies, waits for them, and re-layouts: 8.41 us -> 4.33 us
  Pallas kernels: 86.2 us -> 84.6 us
  other arithmetic: 1.4 us -> 0 us
    pallas_call x1 -> x0, Pallas kernels: 6.58 us -> none  [atom_block(): pl.pallas_call(atom_kernel, in_specs=[smem, smem] + [vmem] * 9, out_specs...]
    pallas_call x1, Pallas kernels: 79.6 us -> 84.6 us  [token_layer(): pl.pallas_call(functools.partial(token_kernel, tuple(names), groups, ring...]
    reshape x4 -> x2, local copies, waits for them, and re-layouts: 3.75 us -> 1.41 us  [per_device(): token_vectors.reshape(-1, groups, width)]
    unnamed x6 -> x2, local copies, waits for them, and re-layouts: 1.44 us -> 2.92 us
    another operation x3 -> x0, other arithmetic: 1.4 us -> none  [rims(): return jnp.stack([array[:RIM], array[array.shape[0] - RIM:]])]
    broadcast_in_dim x1 -> x0, local copies, waits for them, and re-layouts: 1.04 us -> none  [per_device(): jnp.concatenate([owner_rims[0, 0, :RIM], atom_token, owner_rims[1, 0, :RI...]
where the time goes in v2:
time: 89.8 us; the launch traced here: 89.5 us
  Pallas kernels  84.6 us (94%)
  local copies, waits for them, and re-layouts  4.33 us (5%)
    pallas_call x1, Pallas kernels, token_layer(): pl.pallas_call(functools.partial(token_kernel, tuple(names), groups, ring...  84.6 us
    unnamed x2, local copies, waits for them, and re-layouts  2.92 us

profile of v2, /device:TPU:0, one launch (start us, length us, event | category | flops | bytes accessed | tf_op | source)
XLA Modules:
  0.0 89.5 jit_solution(11556992242765540686)
XLA Ops:
  0.6 0.8 reshape.16
  1.4 0.6 copy.23
  2.0 84.6 %token_layer.1 = (bf16[128,768]{1,0:T(8,128)(2,1)}, f32[3,1,1024]{2,1,0:T(1,128)}) custom-call(s32[2,32]{1,0:T(2,128)} %bitcast.28, bf16[128,768]{1,0:T(8,128)(2,1)} %bitcast.20, bf16[128,768]{1,0:T(8,128)(2,1)} %bitcast.21, s32[1,128]{1,0:T(1,128)} %bitcast.29, f32[4,3,192]{2,1,0:T(4,128)} %bitcast.23, s32[8,128]{1,0:T(8,128)} %bitcast.25, ...), custom_call_target="tpu_custom_call" | custom-call | tf_op jit(solution)/shard_map/token_layer/pallas_call | solution.py:690
  86.6 1.6 %copy.26 = bf16[1,128,768]{2,1,0:T(8,128)(2,1)} copy(bf16[1,128,768]{2,1,0:T(8,128)(2,1)} %bitcast.22) | data formatting | bytes 393216
  88.2 1.3 %copy.27 = f32[1,3,1024]{2,0,1:T(1,128)} copy(f32[1,3,1024]{2,0,1:T(1,128)} %bitcast.27) | data formatting | bytes 24576

commit v3 on v2

--- a/solution.py
+++ b/solution.py
@@ -142,20 +142,6 @@
             block, block, self.partner_send.at[at], self.partner_recv.at[at], self.axis, self.partner()
         )
 
-    def greet(self, signal):
-        above, below = self.position > 0, self.position < self.length - 1
-
-        @pl.when(above)
-        def _():
-            signal(self.axis, self.slot(self.position - 1))
-
-        @pl.when(below)
-        def _():
-            signal(self.axis, self.slot(self.position + 1))
-
-        signal(self.axis, self.partner())
-        return jnp.where(above, 1, 0) + jnp.where(below, 1, 0) + 1
-
     def begin(self):
         for side in (0, 1):
 
@@ -210,15 +196,6 @@
         self.index = lax.axis_index(axis)
         self.present = self.index > 0, self.index < size - 1
 
-    def greet(self, signal):
-        for side in (0, 1):
-
-            @pl.when(self.present[side])
-            def _():
-                signal(self.axis, self.index - 1 + 2 * side)
-
-        return jnp.where(self.present[0], 1, 0) + jnp.where(self.present[1], 1, 0)
-
     def copy(self, side):
         at = (self.number, side)
         return remote(
@@ -245,6 +222,28 @@
             def _():
                 self.copy(side).wait_send()
                 self.copy(1 - side).wait_recv()
+
+
+class Spread:
+    def __init__(self, axis, size, view, send, recv, number):
+        self.axis, self.size, self.view = axis, size, view
+        self.send, self.recv, self.number = send, recv, number
+        self.here = lax.axis_index(axis)
+
+    def copy(self, shift, arriving):
+        block = self.view(lax.rem(self.here + self.size - shift, self.size) if arriving else self.here)
+        at = (self.number, shift)
+        peer = lax.rem(self.here + shift, self.size)
+        return remote(block, block, self.send.at[at], self.recv.at[at], self.axis, peer)
+
+    def begin(self):
+        for shift in range(1, self.size):
+            self.copy(shift, False).start()
+
+    def finish(self):
+        for shift in range(1, self.size):
+            self.copy(shift, False).wait_send()
+            self.copy(shift, True).wait_recv()
 
 
 def token_kernel(names, groups, ring, *refs):
@@ -288,12 +287,14 @@
         )
     ]
     kv_flows = [pairs(lambda slot, g=g: r.kv.at[slot, g], g) for g in range(groups)]
-    mask_flow = pairs(lambda slot: r.masks.at[slot], groups)
-    rows_flow = pairs(lambda slot: r.rows_all.at[slot], groups + 1)
+    mask_flow = Spread("seq", ring, lambda slot: r.masks.at[slot], r.spread_send, r.spread_recv, 0)
+    rows_flow = Spread("seq", ring, lambda slot: r.rows_all.at[slot], r.spread_send, r.spread_recv, 1)
 
     for shift in range(1, groups):
         signal("fsdp", lax.rem(me + shift, groups))
-    expected = last + mask_flow.greet(signal) + halos[0].greet(signal)
+    for shift in range(1, ring):
+        signal("seq", lax.rem(seat + shift, ring))
+    expected = last + ring - 1
     for load in loads.values():
         load.start()
 
@@ -348,7 +349,9 @@
     mask_flow.begin()
     for halo in halos:
         halo.begin()
-    offsets = r.vectors[me]
+    offsets = r.vectors[:, :width]
+    for g in range(1, groups):
+        offsets = jnp.where(me == g, r.vectors[:, g * width : (g + 1) * width], offsets)
 
     def adaptive(sample, packed):
         rows_in = r.conds[sample]
@@ -433,7 +436,7 @@
         state = block(0, None)
         if ring > span:
             state = lax.fori_loop(1, ring // span, lambda i, state: block(i * span, state), state)
-        attended = state[2] / state[1]
+        attended = state[2] * (1.0 / state[1])
         result = jnp.zeros((rows, width), jnp.float32)
         for head in range(heads):
             result = result + jnp.where(head_of == head, attended[head * rows : (head + 1) * rows], 0.0)
@@ -443,8 +446,7 @@
     pending = [(transit_chains[g], step) for step in range(last - 1) for g in outer]
     pending += [(flow, step) for step in range(last - 1) for flow in small_chains]
     share = -(-len(pending) // groups)
-    mask_flow.relay()
-    mask_flow.complete()
+    mask_flow.finish()
     loads["bias"].wait()
     kv_flows[inner[0]].relay()
     for number, g in enumerate(inner):
@@ -542,13 +544,12 @@
                     axis=0,
                 )
                 score = matmul_t(stacked, r.atom_key[pl.ds(base, WK), :])
-                masked = r.masked[step * BATCH + i]
-                scores.append(jnp.where(masked > 0.5 * FAR, score * scale + masked, FAR))
+                scores.append(score * scale + r.masked[step * BATCH + i])
             weights = [jnp.exp(score - jnp.max(score, axis=-1, keepdims=True)) for score in scores]
             results = []
             for base, weight in zip(bases, weights):
                 attended = matmul(weight.astype(jnp.bfloat16), r.atom_value[pl.ds(base, WK), :])
-                attended = attended / jnp.sum(weight, axis=-1, keepdims=True)
+                attended = attended * (1.0 / jnp.sum(weight, axis=-1, keepdims=True))
                 result = jnp.zeros((WQ, channels), jnp.float32)
                 for head in range(HA):
                     result = result + jnp.where(
@@ -615,8 +616,7 @@
                 for part in (0, 1):
                     hop(side, g, part).wait_send()
 
-    rows_flow.relay()
-    rows_flow.complete()
+    rows_flow.finish()
     atom_after()
 
 
@@ -675,10 +675,12 @@
         line_recv=dma((chains, 2, hops)),
         act_send=dma((groups,)),
         act_recv=dma((groups,)),
-        seq_send=dma((groups + 2, 2, max(length - 1, 1))),
-        seq_recv=dma((groups + 2, 2, max(length - 1, 1))),
-        hand_send=dma((groups + 2, 2 * length)),
-        hand_recv=dma((groups + 2, 2 * length)),
+        seq_send=dma((groups, 2, max(length - 1, 1))),
+        seq_recv=dma((groups, 2, max(length - 1, 1))),
+        hand_send=dma((groups, 2 * length)),
+        hand_recv=dma((groups, 2 * length)),
+        spread_send=dma((2, ring)),
+        spread_recv=dma((2, ring)),
         halo_send=dma((3, 2)),
         halo_recv=dma((3, 2)),
         swap_send=dma((2,)),
@@ -698,6 +700,23 @@
         ),
         name="token_layer",
     )(bounds, *near.values(), *weights.values())
+
+
+def settle_kernel(token_ref, update_ref, token_out, update_out):
+    token_out[...] = token_ref[...]
+    update_out[...] = update_ref[...]
+
+
+def settle(token, update):
+    vmem = pl.BlockSpec(memory_space=pltpu.VMEM)
+    return pl.pallas_call(
+        settle_kernel,
+        out_shape=tuple(jax.ShapeDtypeStruct(array.shape, array.dtype) for array in (token, update)),
+        in_specs=[vmem] * 2,
+        out_specs=(vmem, vmem),
+        compiler_params=pltpu.CompilerParams(vmem_limit_bytes=VMEM_LIMIT),
+        name="settle",
+    )(token, update)
 
 
 def per_device(
@@ -721,14 +740,12 @@
     atom_vectors,
     position_out,
 ):
-    groups = lax.axis_size("fsdp")
-    width = attention_in.shape[2]
     channels = atom_cond.shape[1]
     near = dict(
         act=token_act[0],
         cond=token_cond[0],
         mask=token_mask[None],
-        vectors=jnp.transpose(token_vectors.reshape(-1, groups, width), (1, 0, 2)),
+        vectors=token_vectors,
         owner=atom_token.reshape(-1, WK),
         owner_ends=atom_token.reshape(-1, 1, WK),
         atom_part=jnp.swapaxes(atom_weights, 1, 2).reshape(-1, channels),
@@ -747,7 +764,7 @@
         skip=atom_skip[0],
         atom_cond=atom_cond,
     )
-    token_result, update = token_layer(near, weights, jnp.swapaxes(window_bounds, 0, 1))
+    token_result, update = settle(*token_layer(near, weights, jnp.swapaxes(window_bounds, 0, 1)))
     return (token_result[None], jnp.transpose(update, (1, 0, 2)))
 
 

time: 89.8 us -> 86 us (0.958)
  local copies, waits for them, and re-layouts: 4.33 us -> 0 us
    unnamed x2 -> x0, local copies, waits for them, and re-layouts: 2.92 us -> none
    pallas_call x0 -> x1, Pallas kernels: none -> 1.62 us  [settle(): pl.pallas_call(settle_kernel, out_shape=tuple((jax.ShapeDtypeStruct(array...]
    reshape x2 -> x0, local copies, waits for them, and re-layouts: 1.41 us -> none  [per_device(): token_vectors.reshape(-1, groups, width)]
    pallas_call x1, Pallas kernels: 84.6 us -> 83.6 us  [token_layer(): pl.pallas_call(functools.partial(token_kernel, tuple(names), groups, ring...]
where the time goes in v3:
time: 86 us; the launch traced here: 85.9 us
  Pallas kernels  85.2 us (99%)
    pallas_call x1, Pallas kernels, token_layer(): pl.pallas_call(functools.partial(token_kernel, tuple(names), groups, ring...  83.6 us

profile of v3, /device:TPU:0, one launch (start us, length us, event | category | flops | bytes accessed | tf_op | source)
XLA Modules:
  0.0 85.9 jit_solution(5894344075953508180)
XLA Ops:
  0.6 83.6 %token_layer.1 = (bf16[128,768]{1,0:T(8,128)(2,1)}, f32[3,1,1024]{2,1,0:T(1,128)}) custom-call(s32[2,32]{1,0:T(2,128)} %bitcast.22, bf16[128,768]{1,0:T(8,128)(2,1)} %bitcast.17, bf16[128,768]{1,0:T(8,128)(2,1)} %bitcast.18, s32[1,128]{1,0:T(1,128)} %bitcast.23, f32[3,768]{1,0:T(4,128)} %refs_4_.1, s32[8,128]{1,0:T(8,128)} %bitcast.20, ...), custom_call_target="tpu_custom_call" | custom-call | tf_op jit(solution)/shard_map/token_layer/pallas_call | solution.py:692
  84.3 1.6 %settle.1 = (bf16[128,768]{1,0:T(8,128)(2,1)}, f32[3,1,1024]{2,1,0:T(1,128)}) custom-call(bf16[128,768]{1,0:T(8,128)(2,1)} %get-tuple-element.6.token_ref, f32[3,1,1024]{2,1,0:T(1,128)} %get-tuple-element.7.update_ref), custom_call_target="tpu_custom_call" | custom-call | tf_op jit(solution)/shard_map/settle/pallas_call | solution.py:712

commit v4 on v3

--- a/solution.py
+++ b/solution.py
@@ -17,6 +17,8 @@
 FAR = -1e30
 RIM = (WK - WQ) // 2
 ATOM_MAPS = 7
+SQUARE = 4
+PARTS = 4
 BATCH = 8
 VMEM_LIMIT = 56 * 1024 * 1024
 MESH = pl.DeviceIdType.MESH
@@ -37,16 +39,6 @@
     return lax.dot_general(
         left_side, right_side, (((1,), (1,)), ((), ())), preferred_element_type=jnp.float32
     )
-
-
-def pack(array):
-    half = array.shape[-2] // 2
-    return jnp.concatenate([array[..., :half, :], array[..., half:, :]], axis=-1)
-
-
-def unpack(array):
-    half = array.shape[-1] // 2
-    return jnp.concatenate([array[..., :half], array[..., half:]], axis=-2)
 
 
 def remote(source, target, send, recv, axis, peer):
@@ -224,6 +216,80 @@
                 self.copy(1 - side).wait_recv()
 
 
+class Plane:
+    def __init__(self, chain, home, send, recv, number):
+        self.chain, self.home, self.send, self.recv, self.number = chain, home, send, recv, number
+        seat = lax.axis_index("seq")
+        self.base = SQUARE * (seat // SQUARE)
+        inside = seat - self.base
+        self.across = lax.axis_index("sample")
+        self.chip, self.core = inside // 2, inside - 2 * (inside // 2)
+
+    def index(self, across, chip, core):
+        return across * SQUARE + chip * 2 + core
+
+    def piece(self, origin, message, across, chip, core):
+        if message in (3, 4):
+            chip = 1 - chip
+        if message in (5, 6):
+            across = 1 - across
+        if message in (7, 8):
+            across, chip = 1 - across, 1 - chip
+        block = self.home.at[origin, self.index(across, chip, core)]
+        half = self.home.shape[-1] // 2
+        if message in (3, 7):
+            block = block.at[:, pl.ds(0, half)]
+        if message in (5, 8):
+            block = block.at[:, pl.ds(half, half)]
+        return block
+
+    def copy(self, step, side, message, arriving):
+        origin = self.chain.here - (step + 1) if side == 0 else self.chain.here + step + 1
+        across, chip, core = self.across, self.chip, self.core
+        if message in (2, 3):
+            axis, peer, sender = "sample", 1 - across, (1 - across, chip, core)
+        elif message in (1, 5):
+            axis, peer = "seq", self.base + 2 * (1 - chip) + core
+            sender = (across, 1 - chip, core)
+        else:
+            axis, peer = "seq", self.base + 2 * chip + 1 - core
+            sender = (across, chip, 1 - core)
+        block = self.piece(origin, message, *(sender if arriving else (across, chip, core)))
+        at = (self.number, 2 * step + side, message)
+        return remote(block, block, self.send.at[at], self.recv.at[at], axis, peer)
+
+    def each(self, step, actions):
+        for side in (0, 1):
+
+            @pl.when(self.chain.guards(side, step)[1])
+            def _():
+                for action, messages in actions:
+                    for message in messages:
+                        if action == "start":
+                            self.copy(step, side, message, False).start()
+                        elif action == "recv":
+                            self.copy(step, side, message, True).wait_recv()
+                        else:
+                            self.copy(step, side, message, False).wait_send()
+
+    def first(self, step):
+        self.each(step, [("start", (1, 2, 0))])
+
+    def second(self, step):
+        self.each(step, [("recv", (1,)), ("start", (3, 4)), ("recv", (2,)), ("start", (5, 6))])
+
+    def third(self, step):
+        self.each(step, [("recv", (3,)), ("start", (7,)), ("recv", (5,)), ("start", (8,))])
+
+    def done(self):
+        for step in range(self.chain.size - 1):
+            self.each(step, [("recv", (0, 4, 6, 7, 8))])
+
+    def drain(self):
+        for step in range(self.chain.size - 1):
+            self.each(step, [("send", tuple(range(9)))])
+
+
 class Spread:
     def __init__(self, axis, size, view, send, recv, number):
         self.axis, self.size, self.view = axis, size, view
@@ -250,9 +316,8 @@
     r = types.SimpleNamespace(**dict(zip(names, refs)))
     me, seat = lax.axis_index("fsdp"), lax.axis_index("seq")
     rows, depth = r.act.shape
-    width = r.ada.shape[1]
+    width = r.attn.shape[1]
     heads = r.bias.shape[0]
-    half = rows // 2
     last = groups - 1
     barrier = pltpu.get_barrier_semaphore()
 
@@ -261,13 +326,17 @@
 
     loads = {
         name: pltpu.make_async_copy(getattr(r, name + "_hbm"), getattr(r, name), r.load.at[number])
-        for number, name in enumerate(("ada", "attn", "bias", "out", "tin", "tout", "atom_bias"))
+        for number, name in enumerate(("attn", "bias", "out", "tin", "tout", "atom_bias"))
     }
     count, channels = r.skip_hbm.shape
     inner_atoms = pl.ds(RIM, count)
     for number, name in enumerate(("skip", "atom_cond")):
         loads[name] = pltpu.make_async_copy(
             getattr(r, name + "_hbm"), getattr(r, name).at[inner_atoms], r.load.at[len(loads)]
+        )
+    for kind in (0, 1):
+        loads[kind] = pltpu.make_async_copy(
+            r.ada_hbm.at[kind], r.ada.at[kind, me], r.load.at[len(loads)]
         )
 
     def pairs(view, *prefix):
@@ -294,27 +363,39 @@
         signal("fsdp", lax.rem(me + shift, groups))
     for shift in range(1, ring):
         signal("seq", lax.rem(seat + shift, ring))
-    expected = last + ring - 1
-    for load in loads.values():
+    across = lax.axis_index("sample")
+    signal("sample", 1 - across)
+    expected = last + ring
+    for load in [loads[0], loads[1]] + [loads[name] for name in loads if name not in (0, 1)]:
         load.start()
 
     def chain(number, view):
         return Chain("fsdp", groups, view, r.line_send, r.line_recv, (number,))
 
-    cond_chains = [
-        chain(part, lambda slot, part=part: r.conds.at[slot, pl.ds(part * half, half)]) for part in (0, 1)
+    inside = seat - SQUARE * (seat // SQUARE)
+    piece = across * SQUARE + inside
+    ada_chains = [chain(kind, lambda slot, kind=kind: r.ada.at[kind, slot, piece]) for kind in (0, 1)]
+    planes = [
+        Plane(flow, r.ada.at[kind], r.plane_send, r.plane_recv, kind)
+        for kind, flow in enumerate(ada_chains)
     ]
-    attend_chains = [chain(2 + g, lambda slot, g=g: r.attend.at[slot, g]) for g in range(groups)]
-    transit_chains = [
-        chain(2 + groups + g, lambda slot, g=g: r.transit.at[slot, g]) for g in range(groups)
-    ]
+    part_rows = rows // PARTS
+
+    def row_chains(ref, first):
+        return [
+            chain(first + part, lambda slot, part=part: ref.at[slot, pl.ds(part * part_rows, part_rows)])
+            for part in range(PARTS)
+        ]
+
+    attend_chains = row_chains(r.attend, 2)
+    transit_chains = row_chains(r.transit, 2 + PARTS)
     parity = seat - 2 * (seat // 2)
     atom_half, project_half = r.atom_part.shape[0] // 2, r.project_part.shape[0] // 2
     atom_rows = pl.ds(pl.multiple_of(parity * atom_half, 16), atom_half)
     project_rows = pl.ds(pl.multiple_of(parity * project_half, 16), project_half)
     small_chains = [
-        chain(2 + 2 * groups, lambda slot: r.atom_all.at[slot, atom_rows]),
-        chain(3 + 2 * groups, lambda slot: r.project.at[slot, project_rows]),
+        chain(2 + 2 * PARTS, lambda slot: r.atom_all.at[slot, atom_rows]),
+        chain(3 + 2 * PARTS, lambda slot: r.project.at[slot, project_rows]),
     ]
 
     def swaps():
@@ -325,86 +406,68 @@
             for i, block in enumerate(blocks)
         ]
 
-    r.conds[me] = layer_norm(r.cond[...]).astype(jnp.bfloat16)
+    order, found = [me] + [0] * last, 1
+    for distance in range(1, groups):
+        for sample in (me - distance, me + distance):
+            valid = (sample >= 0) & (sample <= last)
+            for n in range(1, groups):
+                order[n] = jnp.where(valid & (found == n), sample, order[n])
+            found = found + jnp.where(valid, 1, 0)
+
+    pl.semaphore_wait(barrier, expected)
+    loads[0].wait()
+    ada_chains[0].begin()
     r.masks[seat] = r.mask[...]
+    r.cond_normed[...] = layer_norm(r.cond[...]).astype(jnp.bfloat16)
+    r.act_normed[...] = layer_norm(r.act[...])
     r.atom_all[me, atom_rows] = r.atom_part[atom_rows, :]
     r.project[me, project_rows] = r.project_part[project_rows, :]
-    pl.semaphore_wait(barrier, expected)
-    for flow in cond_chains:
+    for step in range(last):
+        ada_chains[0].arrive(step)
+        planes[0].first(step)
+        if step > 0:
+            planes[0].second(step - 1)
+    loads[1].wait()
+    ada_chains[1].begin()
+    planes[0].second(last - 1)
+    for step in range(last):
+        planes[0].third(step)
+        if step < last - 1:
+            ada_chains[1].arrive(step)
+            planes[1].first(step)
+    planes[0].done()
+
+    def adaptive(kind, target):
+        pieces = []
+        for g in range(groups):
+            columns = slice(g * width, (g + 1) * width)
+            maps = r.ada[kind, g].reshape(2 * width, depth)
+            both = matmul_t(r.cond_normed[...], maps)
+            gate = jax.nn.sigmoid(both[:, :width] + r.vectors[kind : kind + 1, columns])
+            pieces.append((gate * r.act_normed[:, columns] + both[:, width:]).astype(jnp.bfloat16))
+        target[me] = jnp.concatenate(pieces, axis=1)
+
+    adaptive(0, r.attend)
+    for flow in attend_chains:
         flow.begin()
-    act_normed = layer_norm(r.act[...]).astype(jnp.bfloat16)
-    for g in range(groups):
-        r.act_out[g] = pack(act_normed[:, g * width : (g + 1) * width])
-
-    def slots(shift, arriving):
-        peer = lax.rem(me + shift, groups)
-        landing = lax.rem(me + groups - shift, groups) if arriving else me
-        return remote(
-            r.act_out.at[peer], r.acts.at[landing], r.act_send.at[shift], r.act_recv.at[shift],
-            "fsdp", peer,
-        )
-
-    for shift in range(1, groups):
-        slots(shift, False).start()
+    ada_chains[1].arrive(last - 1)
+    planes[1].first(last - 1)
     mask_flow.begin()
     for halo in halos:
         halo.begin()
-    offsets = r.vectors[:, :width]
+    for step in range(last - 1):
+        planes[1].second(step)
+    query_bias = r.vectors[2:3, :width]
     for g in range(1, groups):
-        offsets = jnp.where(me == g, r.vectors[:, g * width : (g + 1) * width], offsets)
-
-    def adaptive(sample, packed):
-        rows_in = r.conds[sample]
-        values = unpack(packed).astype(jnp.float32)
-
-        def one(scale, shift, vector):
-            gate = jax.nn.sigmoid(matmul_t(rows_in, r.ada[scale]) + offsets[vector : vector + 1, :])
-            return pack((gate * values + matmul_t(rows_in, r.ada[shift])).astype(jnp.bfloat16))
-
-        r.attend[me, sample] = one(0, 1, 0)
-        r.transit[me, sample] = one(2, 3, 1)
-
-    loads["ada"].wait()
-    adaptive(me, r.act_out[me])
-    inner = sorted(range(groups), key=lambda g: max(g, last - g))
-    outer = sorted(range(groups), key=lambda g: (-max(g, last - g), g))
-    for step in range(last):
-        for flow in cond_chains:
-            flow.arrive(step)
-        for side in (0, 1):
-
-            @pl.when(cond_chains[0].guards(side, step)[1])
-            def _():
-                origin = me - (step + 1) if side == 0 else me + step + 1
-                slots(step + 1 if side == 0 else last - step, True).wait_recv()
-                adaptive(origin, r.acts[origin])
-
-        for g in inner:
-            if max(g, last - g) == step + 1:
-                attend_chains[g].begin()
-
-    def joined(ref, g):
-        return jnp.concatenate([unpack(ref[origin, g]) for origin in range(groups)], axis=1)
-
-    def projections(g):
-        full = joined(r.attend, g)
-        r.queries[g] = (matmul_t(full, r.attn[0]) + offsets[2:3, :]).astype(jnp.bfloat16)
+        query_bias = jnp.where(me == g, r.vectors[2:3, g * width : (g + 1) * width], query_bias)
+
+    def projections(n):
+        full = r.attend[order[n]]
         both = r.attn[1:3].reshape(2 * width, depth)
-        r.kv[seat, g] = matmul_t(full, both).astype(jnp.bfloat16)
-        kv_flows[g].begin()
-        r.gates[g] = matmul_t(full, r.attn[3]).astype(jnp.bfloat16)
-
-    for step in range(last - 1):
-        for g in inner:
-            attend_chains[g].arrive(step)
-    for g in outer:
-        transit_chains[g].begin()
-    loads["attn"].wait()
-    for g in inner:
-        attend_chains[g].arrive(last - 1)
-        projections(g)
-    for flow in small_chains:
-        flow.begin()
+        r.kv[seat, n] = matmul_t(full, both).astype(jnp.bfloat16)
+        kv_flows[n].begin()
+        r.queries[n] = (matmul_t(full, r.attn[0]) + query_bias).astype(jnp.bfloat16)
+        r.gates[n] = matmul_t(full, r.attn[3]).astype(jnp.bfloat16)
 
     def attention(g):
         queries = r.queries[g]
@@ -443,22 +506,40 @@
         gate = jax.nn.sigmoid(r.gates[g].astype(jnp.float32))
         r.gated[g] = (result * gate).astype(jnp.bfloat16)
 
-    pending = [(transit_chains[g], step) for step in range(last - 1) for g in outer]
-    pending += [(flow, step) for step in range(last - 1) for flow in small_chains]
-    share = -(-len(pending) // groups)
+    def attend_group(n):
+        kv_flows[n].relay()
+        kv_flows[n].complete()
+        attention(n)
+
+    for flow in attend_chains:
+        flow.arrive(0)
+    planes[1].second(last - 1)
+    for step in range(last):
+        planes[1].third(step)
+    planes[1].done()
+    adaptive(1, r.transit)
+    loads["attn"].wait()
+    projections(0)
+    projections(1)
+    for step in range(1, last - 1):
+        for flow in attend_chains:
+            flow.arrive(step)
+        projections(step + 1)
+    for flow in transit_chains:
+        flow.begin()
     mask_flow.finish()
     loads["bias"].wait()
-    kv_flows[inner[0]].relay()
-    for number, g in enumerate(inner):
-        if number + 1 < groups:
-            kv_flows[inner[number + 1]].relay()
-        kv_flows[g].complete()
-        attention(g)
-        for flow, step in pending[number * share : (number + 1) * share]:
-            flow.arrive(step)
+    attend_group(0)
+    if last > 1:
+        for flow in attend_chains:
+            flow.arrive(last - 1)
+        projections(last)
+    attend_group(1)
+    for flow in small_chains:
+        flow.begin()
 
     def hop(side, g, part):
-        piece = pl.ds(part * half, half)
+        piece = pl.ds(part * part_rows, part_rows)
         at = (side, g, part)
         return remote(
             r.sums_out.at[g, piece], r.sums_in.at[side, g, piece], r.sum_send.at[at], r.sum_recv.at[at],
@@ -467,21 +548,35 @@
 
     def take(side, g, part):
         hop(side, g, part).wait_recv()
-        piece = pl.ds(part * half, half)
+        piece = pl.ds(part * part_rows, part_rows)
         r.total[g, piece] += r.sums_in[side, g, piece].astype(jnp.float32)
 
-    def reduce(stage, g):
-        for side, here, goes in ((0, stage, g > stage), (1, last - stage, g < last - stage)):
-            if goes:
-
-                @pl.when(me == here)
-                def _():
-                    for part in (0, 1):
-                        piece = pl.ds(part * half, half)
-                        if stage > 0:
-                            take(side, g, part)
-                        r.sums_out[g, piece] = r.total[g, piece].astype(jnp.bfloat16)
-                        hop(side, g, part).start()
+    def send(side, g, part):
+        piece = pl.ds(part * part_rows, part_rows)
+        r.sums_out[g, piece] = r.total[g, piece].astype(jnp.bfloat16)
+        hop(side, g, part).start()
+
+    def transition(n):
+        g = order[n]
+        full = r.transit[g]
+        hidden = jax.nn.silu(matmul(full, r.tin[0])) * matmul(full, r.tin[1])
+        r.total[g] = matmul(r.gated[n], r.out[...]) + matmul(hidden.astype(jnp.bfloat16), r.tout[...])
+        for side, goes in ((0, (me == 0) & (g > 0)), (1, (me == last) & (g < last))):
+
+            @pl.when(goes)
+            def _():
+                for part in range(PARTS):
+                    send(side, g, part)
+
+    def reduce(stage):
+        for side, here in ((0, stage), (1, last - stage)):
+
+            @pl.when(me == here)
+            def _():
+                for g in range(here + 1, groups) if side == 0 else range(here - 1, -1, -1):
+                    for part in range(PARTS):
+                        take(side, g, part)
+                        send(side, g, part)
 
     heads_out = lax.broadcasted_iota(jnp.int32, (WQ, channels), 1) // (channels // HA)
     tokens = ring * rows
@@ -570,14 +665,13 @@
 
     for name in ("out", "tin", "tout"):
         loads[name].wait()
-    for g in outer:
-        transit_chains[g].arrive(last - 1)
-        full = joined(r.transit, g)
-        hidden = jax.nn.silu(matmul(full, r.tin[0])) * matmul(full, r.tin[1])
-        r.total[g] = matmul(r.gated[g], r.out[...]) + matmul(hidden.astype(jnp.bfloat16), r.tout[...])
-        reduce(0, g)
-    for flow in small_chains:
-        flow.arrive(last - 1)
+    transition(0)
+    for step in range(last):
+        for flow in transit_chains + small_chains:
+            flow.arrive(step)
+        if step + 2 < groups:
+            attend_group(step + 2)
+        transition(step + 1)
     for copy in swaps():
         copy.start()
     for name in ("skip", "atom_cond", "atom_bias"):
@@ -587,8 +681,7 @@
     for copy in swaps():
         copy.wait()
     for stage in range(1, last):
-        for g in outer:
-            reduce(stage, g)
+        reduce(stage)
         if stage == 1:
             atom_before()
     if last == 1:
@@ -597,23 +690,21 @@
 
         @pl.when(present)
         def _():
-            for part in (0, 1):
+            for part in range(PARTS):
                 take(side, me, part)
 
     token = (r.act[...].astype(jnp.float32) + r.total[me]).astype(jnp.bfloat16)
     r.token[...] = token
     r.rows_all[seat] = matmul(token, r.project[...].reshape(depth, -1)).astype(jnp.bfloat16)
     rows_flow.begin()
-    for flow in cond_chains + attend_chains + transit_chains + small_chains:
+    for flow in ada_chains + planes + attend_chains + transit_chains + small_chains:
         flow.drain()
-    for shift in range(1, groups):
-        slots(shift, False).wait_send()
     for g in range(groups):
         for side, goes in ((0, g > me), (1, g < me)):
 
             @pl.when(goes)
             def _():
-                for part in (0, 1):
+                for part in range(PARTS):
                     hop(side, g, part).wait_send()
 
     rows_flow.finish()
@@ -623,7 +714,7 @@
 def token_layer(near, weights, bounds):
     groups, ring = lax.axis_size("fsdp"), lax.axis_size("seq")
     rows, depth = near["act"].shape
-    width = weights["ada"].shape[1]
+    width = weights["attn"].shape[1]
     count, channels = weights["skip"].shape
     extended = count + 2 * RIM
     dma = pltpu.SemaphoreType.DMA
@@ -634,8 +725,7 @@
         token=((rows, depth), half_type),
         update=((near["position"].shape[0], 1, count), jnp.float32),
     )
-    packed = (groups, groups, rows // 2, 2 * width)
-    chains = 4 + 2 * groups
+    chains = 4 + 2 * PARTS
     hops = max(groups - 1, 1)
     length = ring // 2
     scratch = {name: pltpu.VMEM(array.shape, array.dtype) for name, array in weights.items()}
@@ -656,11 +746,11 @@
         owner_rims=pltpu.VMEM((2, 1, near["owner"].shape[1]), jnp.int32),
         rows_all=pltpu.VMEM((ring, rows, channels), half_type),
         atom_all=pltpu.VMEM((groups,) + atom_part.shape, half_type),
-        conds=pltpu.VMEM((groups, rows, depth), half_type),
-        act_out=pltpu.VMEM(packed[1:], half_type),
-        acts=pltpu.VMEM(packed[1:], half_type),
-        attend=pltpu.VMEM(packed, half_type),
-        transit=pltpu.VMEM(packed, half_type),
+        ada=pltpu.VMEM((2, groups) + weights["ada"].shape[1:], half_type),
+        cond_normed=pltpu.VMEM((rows, depth), half_type),
+        act_normed=pltpu.VMEM((rows, depth), jnp.float32),
+        attend=pltpu.VMEM((groups, rows, depth), half_type),
+        transit=pltpu.VMEM((groups, rows, depth), half_type),
         queries=pltpu.VMEM((groups, rows, width), half_type),
         gates=pltpu.VMEM((groups, rows, width), half_type),
         gated=pltpu.VMEM((groups, rows, width), half_type),
@@ -670,11 +760,11 @@
         total=pltpu.VMEM((groups, rows, depth), jnp.float32),
         sums_out=pltpu.VMEM((groups, rows, depth), half_type),
         sums_in=pltpu.VMEM((2, groups, rows, depth), half_type),
-        load=dma((len(weights),)),
+        load=dma((len(weights) + 1,)),
         line_send=dma((chains, 2, hops)),
         line_recv=dma((chains, 2, hops)),
-        act_send=dma((groups,)),
-        act_recv=dma((groups,)),
+        plane_send=dma((2, 2 * hops, 9)),
+        plane_recv=dma((2, 2 * hops, 9)),
         seq_send=dma((groups, 2, max(length - 1, 1))),
         seq_recv=dma((groups, 2, max(length - 1, 1))),
         hand_send=dma((groups, 2 * length)),
@@ -685,8 +775,8 @@
         halo_recv=dma((3, 2)),
         swap_send=dma((2,)),
         swap_recv=dma((2,)),
-        sum_send=dma((2, groups, 2)),
-        sum_recv=dma((2, groups, 2)),
+        sum_send=dma((2, groups, PARTS)),
+        sum_recv=dma((2, groups, PARTS)),
     )
     names = ["bounds"] + list(near) + [name + "_hbm" for name in weights] + list(outs) + list(scratch)
     return pl.pallas_call(
@@ -741,6 +831,7 @@
     position_out,
 ):
     channels = atom_cond.shape[1]
+    helpers = SQUARE * lax.axis_size("sample")
     near = dict(
         act=token_act[0],
         cond=token_cond[0],
@@ -754,7 +845,7 @@
         position=position_out,
     )
     weights = dict(
-        ada=jnp.swapaxes(ada_weights, 1, 2),
+        ada=jnp.swapaxes(ada_weights, 1, 2).reshape(2, helpers, -1, ada_weights.shape[1]),
         attn=jnp.swapaxes(attention_in, 1, 2),
         bias=pair_bias,
         out=attention_out,

time: 86 us -> 87 us (1.012)
  Pallas kernels: 85.2 us -> 86.2 us
    pallas_call x1, Pallas kernels: 83.6 us -> 84.6 us  [token_layer(): pl.pallas_call(functools.partial(token_kernel, tuple(names), groups, ring...]
where the time goes in v4:
time: 87 us; the launch traced here: 86.9 us
  Pallas kernels  86.2 us (99%)
    pallas_call x1, Pallas kernels, token_layer(): pl.pallas_call(functools.partial(token_kernel, tuple(names), groups, ring...  84.6 us

profile of v4, /device:TPU:0, one launch (start us, length us, event | category | flops | bytes accessed | tf_op | source)
XLA Modules:
  0.0 86.9 jit_solution(1641621774860396519)
XLA Ops:
  0.6 84.6 %token_layer.1 = (bf16[128,768]{1,0:T(8,128)(2,1)}, f32[3,1,1024]{2,1,0:T(1,128)}) custom-call(s32[2,32]{1,0:T(2,128)} %bitcast.24, bf16[128,768]{1,0:T(8,128)(2,1)} %bitcast.19, bf16[128,768]{1,0:T(8,128)(2,1)} %bitcast.20, s32[1,128]{1,0:T(1,128)} %bitcast.25, f32[3,768]{1,0:T(4,128)} %refs_4_.1, s32[8,128]{1,0:T(8,128)} %bitcast.22, ...), custom_call_target="tpu_custom_call" | custom-call | tf_op jit(solution)/shard_map/token_layer/pallas_call | solution.py:782
  85.2 1.6 %settle.1 = (bf16[128,768]{1,0:T(8,128)(2,1)}, f32[3,1,1024]{2,1,0:T(1,128)}) custom-call(bf16[128,768]{1,0:T(8,128)(2,1)} %get-tuple-element.6.token_ref, f32[3,1,1024]{2,1,0:T(1,128)} %get-tuple-element.7.update_ref), custom_call_target="tpu_custom_call" | custom-call | tf_op jit(solution)/shard_map/settle/pallas_call | solution.py:802

commit v5 on v4

--- a/solution.py
+++ b/solution.py
@@ -374,9 +374,19 @@
 
     inside = seat - SQUARE * (seat // SQUARE)
     piece = across * SQUARE + inside
-    ada_chains = [chain(kind, lambda slot, kind=kind: r.ada.at[kind, slot, piece]) for kind in (0, 1)]
+    cut = depth // 2
+    ada_chains = [
+        [
+            chain(
+                2 * kind + side,
+                lambda slot, kind=kind, side=side: r.ada.at[kind, slot, piece, :, pl.ds(side * cut, cut)],
+            )
+            for side in (0, 1)
+        ]
+        for kind in (0, 1)
+    ]
     planes = [
-        Plane(flow, r.ada.at[kind], r.plane_send, r.plane_recv, kind)
+        Plane(flow[0], r.ada.at[kind], r.plane_send, r.plane_recv, kind)
         for kind, flow in enumerate(ada_chains)
     ]
     part_rows = rows // PARTS
@@ -387,15 +397,15 @@
             for part in range(PARTS)
         ]
 
-    attend_chains = row_chains(r.attend, 2)
-    transit_chains = row_chains(r.transit, 2 + PARTS)
+    attend_chains = row_chains(r.attend, 4)
+    transit_chains = row_chains(r.transit, 4 + PARTS)
     parity = seat - 2 * (seat // 2)
     atom_half, project_half = r.atom_part.shape[0] // 2, r.project_part.shape[0] // 2
     atom_rows = pl.ds(pl.multiple_of(parity * atom_half, 16), atom_half)
     project_rows = pl.ds(pl.multiple_of(parity * project_half, 16), project_half)
     small_chains = [
-        chain(2 + 2 * PARTS, lambda slot: r.atom_all.at[slot, atom_rows]),
-        chain(3 + 2 * PARTS, lambda slot: r.project.at[slot, project_rows]),
+        chain(4 + 2 * PARTS, lambda slot: r.atom_all.at[slot, atom_rows]),
+        chain(5 + 2 * PARTS, lambda slot: r.project.at[slot, project_rows]),
     ]
 
     def swaps():
@@ -416,24 +426,28 @@
 
     pl.semaphore_wait(barrier, expected)
     loads[0].wait()
-    ada_chains[0].begin()
+    for flow in ada_chains[0]:
+        flow.begin()
     r.masks[seat] = r.mask[...]
     r.cond_normed[...] = layer_norm(r.cond[...]).astype(jnp.bfloat16)
     r.act_normed[...] = layer_norm(r.act[...])
     r.atom_all[me, atom_rows] = r.atom_part[atom_rows, :]
     r.project[me, project_rows] = r.project_part[project_rows, :]
     for step in range(last):
-        ada_chains[0].arrive(step)
+        for flow in ada_chains[0]:
+            flow.arrive(step)
         planes[0].first(step)
         if step > 0:
             planes[0].second(step - 1)
     loads[1].wait()
-    ada_chains[1].begin()
+    for flow in ada_chains[1]:
+        flow.begin()
     planes[0].second(last - 1)
     for step in range(last):
         planes[0].third(step)
         if step < last - 1:
-            ada_chains[1].arrive(step)
+            for flow in ada_chains[1]:
+                flow.arrive(step)
             planes[1].first(step)
     planes[0].done()
 
@@ -450,13 +464,13 @@
     adaptive(0, r.attend)
     for flow in attend_chains:
         flow.begin()
-    ada_chains[1].arrive(last - 1)
+    for flow in ada_chains[1]:
+        flow.arrive(last - 1)
     planes[1].first(last - 1)
+    planes[1].second(0)
     mask_flow.begin()
     for halo in halos:
         halo.begin()
-    for step in range(last - 1):
-        planes[1].second(step)
     query_bias = r.vectors[2:3, :width]
     for g in range(1, groups):
         query_bias = jnp.where(me == g, r.vectors[2:3, g * width : (g + 1) * width], query_bias)
@@ -513,27 +527,28 @@
 
     for flow in attend_chains:
         flow.arrive(0)
-    planes[1].second(last - 1)
-    for step in range(last):
+    for step in range(1, last):
+        planes[1].second(step)
+    for step in range(last - 1):
         planes[1].third(step)
-    planes[1].done()
-    adaptive(1, r.transit)
-    loads["attn"].wait()
-    projections(0)
-    projections(1)
     for step in range(1, last - 1):
         for flow in attend_chains:
             flow.arrive(step)
-        projections(step + 1)
+    planes[1].third(last - 1)
+    planes[1].done()
+    adaptive(1, r.transit)
     for flow in transit_chains:
         flow.begin()
+    loads["attn"].wait()
+    for n in range(last):
+        projections(n)
+    if last > 1:
+        for flow in attend_chains:
+            flow.arrive(last - 1)
+    projections(last)
     mask_flow.finish()
     loads["bias"].wait()
     attend_group(0)
-    if last > 1:
-        for flow in attend_chains:
-            flow.arrive(last - 1)
-        projections(last)
     attend_group(1)
     for flow in small_chains:
         flow.begin()
@@ -556,27 +571,52 @@
         r.sums_out[g, piece] = r.total[g, piece].astype(jnp.bfloat16)
         hop(side, g, part).start()
 
-    def transition(n):
+    def far(number, size):
+        piece = pl.ds(number * size, size)
+        return remote(
+            r.sums_out.at[last - me, piece], r.sums_far.at[piece], r.far_send.at[number],
+            r.far_recv.at[number], "fsdp", last - me,
+        )
+
+    half = rows // 2
+
+    def transition(n, number, size):
         g = order[n]
-        full = r.transit[g]
+        piece = pl.ds(number * size, size)
+        parts = range(number * size // part_rows, (number + 1) * size // part_rows)
+        full = r.transit[g, piece]
         hidden = jax.nn.silu(matmul(full, r.tin[0])) * matmul(full, r.tin[1])
-        r.total[g] = matmul(r.gated[n], r.out[...]) + matmul(hidden.astype(jnp.bfloat16), r.tout[...])
-        for side, goes in ((0, (me == 0) & (g > 0)), (1, (me == last) & (g < last))):
-
-            @pl.when(goes)
-            def _():
-                for part in range(PARTS):
+        sums = matmul(r.gated[n, piece], r.out[...])
+        r.total[g, piece] = sums + matmul(hidden.astype(jnp.bfloat16), r.tout[...])
+        ends = ((0, 0, last, 1), (1, last, 0, last - 1))
+        for side, end, other, next_to_end in ends:
+            beyond = g > me if side == 0 else g < me
+            begins = (me == end) & beyond & (g != other)
+            if last > 1:
+                begins = begins | ((me == next_to_end) & (g == other))
+
+            @pl.when(begins)
+            def _():
+                for part in parts:
                     send(side, g, part)
 
+        if n == last:
+
+            @pl.when(((me == 0) & (g == last)) | ((me == last) & (g == 0)))
+            def _():
+                r.sums_out[g, piece] = r.total[g, piece].astype(jnp.bfloat16)
+                far(number, size).start()
+
     def reduce(stage):
-        for side, here in ((0, stage), (1, last - stage)):
+        for side, here, other in ((0, stage, last), (1, last - stage, 0)):
 
             @pl.when(me == here)
             def _():
                 for g in range(here + 1, groups) if side == 0 else range(here - 1, -1, -1):
-                    for part in range(PARTS):
-                        take(side, g, part)
-                        send(side, g, part)
+                    if stage > 1 or g != other:
+                        for part in range(PARTS):
+                            take(side, g, part)
+                            send(side, g, part)
 
     heads_out = lax.broadcasted_iota(jnp.int32, (WQ, channels), 1) // (channels // HA)
     tokens = ring * rows
@@ -665,42 +705,57 @@
 
     for name in ("out", "tin", "tout"):
         loads[name].wait()
-    transition(0)
-    for step in range(last):
+    transition(0, 0, rows)
+    for step in range(last - 1):
         for flow in transit_chains + small_chains:
             flow.arrive(step)
-        if step + 2 < groups:
-            attend_group(step + 2)
-        transition(step + 1)
+        attend_group(step + 2)
+        transition(step + 1, 0, rows)
+    for number in (0, 1):
+        for flow in transit_chains[number * PARTS // 2 : (number + 1) * PARTS // 2]:
+            flow.arrive(last - 1)
+        transition(last, number, half)
+    for flow in small_chains:
+        flow.arrive(last - 1)
     for copy in swaps():
         copy.start()
+    for stage in range(1, last):
+        reduce(stage)
     for name in ("skip", "atom_cond", "atom_bias"):
         loads[name].wait()
     for halo in halos:
         halo.finish()
     for copy in swaps():
         copy.wait()
-    for stage in range(1, last):
-        reduce(stage)
-        if stage == 1:
-            atom_before()
-    if last == 1:
-        atom_before()
-    for side, present in ((0, me > 0), (1, me < last)):
-
-        @pl.when(present)
-        def _():
-            for part in range(PARTS):
-                take(side, me, part)
+    atom_before()
+    if last > 1:
+        for side, present in ((0, me > 0), (1, me < last)):
+
+            @pl.when(present)
+            def _():
+                for part in range(PARTS):
+                    take(side, me, part)
+
+    @pl.when((me == 0) | (me == last))
+    def _():
+        for number in (0, 1):
+            far(number, half).wait_recv()
+        r.total[me] += r.sums_far[...].astype(jnp.float32)
 
     token = (r.act[...].astype(jnp.float32) + r.total[me]).astype(jnp.bfloat16)
     r.token[...] = token
     r.rows_all[seat] = matmul(token, r.project[...].reshape(depth, -1)).astype(jnp.bfloat16)
     rows_flow.begin()
-    for flow in ada_chains + planes + attend_chains + transit_chains + small_chains:
+
+    @pl.when((me == 0) | (me == last))
+    def _():
+        for number in (0, 1):
+            far(number, half).wait_send()
+
+    for flow in ada_chains[0] + ada_chains[1] + planes + attend_chains + transit_chains + small_chains:
         flow.drain()
     for g in range(groups):
-        for side, goes in ((0, g > me), (1, g < me)):
+        for side, goes in ((0, (g > me) & (g - me < last)), (1, (g < me) & (me - g < last))):
 
             @pl.when(goes)
             def _():
@@ -725,7 +780,7 @@
         token=((rows, depth), half_type),
         update=((near["position"].shape[0], 1, count), jnp.float32),
     )
-    chains = 4 + 2 * PARTS
+    chains = 6 + 2 * PARTS
     hops = max(groups - 1, 1)
     length = ring // 2
     scratch = {name: pltpu.VMEM(array.shape, array.dtype) for name, array in weights.items()}
@@ -775,6 +830,9 @@
         halo_recv=dma((3, 2)),
         swap_send=dma((2,)),
         swap_recv=dma((2,)),
+        sums_far=pltpu.VMEM((rows, depth), half_type),
+        far_send=dma((2,)),
+        far_recv=dma((2,)),
         sum_send=dma((2, groups, PARTS)),
         sum_recv=dma((2, groups, PARTS)),
     )

time: 87 us -> 86.6 us (level)
  no operation moved by 1% of the time
where the time goes in v5:
time: 86.6 us; the launch traced here: 86.5 us
  Pallas kernels  85.8 us (99%)
    pallas_call x1, Pallas kernels, token_layer(): pl.pallas_call(functools.partial(token_kernel, tuple(names), groups, ring...  84.2 us

profile of v5, /device:TPU:0, one launch (start us, length us, event | category | flops | bytes accessed | tf_op | source)
XLA Modules:
  0.0 86.5 jit_solution(8676556221496217343)
XLA Ops:
  0.6 84.2 %token_layer.1 = (bf16[128,768]{1,0:T(8,128)(2,1)}, f32[3,1,1024]{2,1,0:T(1,128)}) custom-call(s32[2,32]{1,0:T(2,128)} %bitcast.24, bf16[128,768]{1,0:T(8,128)(2,1)} %bitcast.19, bf16[128,768]{1,0:T(8,128)(2,1)} %bitcast.20, s32[1,128]{1,0:T(1,128)} %bitcast.25, f32[3,768]{1,0:T(4,128)} %refs_4_.1, s32[8,128]{1,0:T(8,128)} %bitcast.22, ...), custom_call_target="tpu_custom_call" | custom-call | tf_op jit(solution)/shard_map/token_layer/pallas_call | solution.py:840
  84.8 1.6 %settle.1 = (bf16[128,768]{1,0:T(8,128)(2,1)}, f32[3,1,1024]{2,1,0:T(1,128)}) custom-call(bf16[128,768]{1,0:T(8,128)(2,1)} %get-tuple-element.6.token_ref, f32[3,1,1024]{2,1,0:T(1,128)} %get-tuple-element.7.update_ref), custom_call_target="tpu_custom_call" | custom-call | tf_op jit(solution)/shard_map/settle/pallas_call | solution.py:860

commit v6 on v3

--- a/solution.py
+++ b/solution.py
@@ -17,6 +17,8 @@
 FAR = -1e30
 RIM = (WK - WQ) // 2
 ATOM_MAPS = 7
+SQUARE = 4
+PARTS = 4
 BATCH = 8
 VMEM_LIMIT = 56 * 1024 * 1024
 MESH = pl.DeviceIdType.MESH
@@ -253,6 +255,7 @@
     width = r.ada.shape[1]
     heads = r.bias.shape[0]
     half = rows // 2
+    part_rows = rows // PARTS
     last = groups - 1
     barrier = pltpu.get_barrier_semaphore()
 
@@ -308,26 +311,37 @@
     transit_chains = [
         chain(2 + groups + g, lambda slot, g=g: r.transit.at[slot, g]) for g in range(groups)
     ]
-    parity = seat - 2 * (seat // 2)
-    atom_half, project_half = r.atom_part.shape[0] // 2, r.project_part.shape[0] // 2
-    atom_rows = pl.ds(pl.multiple_of(parity * atom_half, 16), atom_half)
-    project_rows = pl.ds(pl.multiple_of(parity * project_half, 16), project_half)
+    base = SQUARE * (seat // SQUARE)
+    inside = seat - base
+    atom_quarter, project_quarter = r.atom_pad.shape[0] // SQUARE, r.project_part.shape[0] // SQUARE
+
+    def quarters(number):
+        return (
+            pl.ds(pl.multiple_of(number * atom_quarter, 16), atom_quarter),
+            pl.ds(pl.multiple_of(number * project_quarter, 16), project_quarter),
+        )
+
+    atom_rows, project_rows = quarters(inside)
     small_chains = [
         chain(2 + 2 * groups, lambda slot: r.atom_all.at[slot, atom_rows]),
         chain(3 + 2 * groups, lambda slot: r.project.at[slot, project_rows]),
     ]
 
-    def swaps():
-        partner = seat + 1 - 2 * parity
-        blocks = (r.atom_all.at[:, atom_rows], r.project.at[:, project_rows])
+    def swaps(shift, arriving):
+        peer = base + lax.rem(inside + shift, SQUARE)
+        ones, others = quarters(lax.rem(inside + SQUARE - shift, SQUARE) if arriving else inside)
+        blocks = (r.atom_all.at[:, ones], r.project.at[:, others])
         return [
-            remote(block, block, r.swap_send.at[i], r.swap_recv.at[i], "seq", partner)
+            remote(block, block, r.swap_send.at[i, shift], r.swap_recv.at[i, shift], "seq", peer)
             for i, block in enumerate(blocks)
         ]
 
     r.conds[me] = layer_norm(r.cond[...]).astype(jnp.bfloat16)
     r.masks[seat] = r.mask[...]
-    r.atom_all[me, atom_rows] = r.atom_part[atom_rows, :]
+    height = r.atom_part.shape[0]
+    r.atom_pad[0:height] = r.atom_part[...]
+    r.atom_pad[height:] = jnp.zeros((r.atom_pad.shape[0] - height, channels), jnp.bfloat16)
+    r.atom_all[me, atom_rows] = r.atom_pad[atom_rows, :]
     r.project[me, project_rows] = r.project_part[project_rows, :]
     pl.semaphore_wait(barrier, expected)
     for flow in cond_chains:
@@ -458,7 +472,7 @@
             flow.arrive(step)
 
     def hop(side, g, part):
-        piece = pl.ds(part * half, half)
+        piece = pl.ds(part * part_rows, part_rows)
         at = (side, g, part)
         return remote(
             r.sums_out.at[g, piece], r.sums_in.at[side, g, piece], r.sum_send.at[at], r.sum_recv.at[at],
@@ -467,7 +481,7 @@
 
     def take(side, g, part):
         hop(side, g, part).wait_recv()
-        piece = pl.ds(part * half, half)
+        piece = pl.ds(part * part_rows, part_rows)
         r.total[g, piece] += r.sums_in[side, g, piece].astype(jnp.float32)
 
     def reduce(stage, g):
@@ -476,8 +490,8 @@
 
                 @pl.when(me == here)
                 def _():
-                    for part in (0, 1):
-                        piece = pl.ds(part * half, half)
+                    for part in range(PARTS):
+                        piece = pl.ds(part * part_rows, part_rows)
                         if stage > 0:
                             take(side, g, part)
                         r.sums_out[g, piece] = r.total[g, piece].astype(jnp.bfloat16)
@@ -578,26 +592,27 @@
         reduce(0, g)
     for flow in small_chains:
         flow.arrive(last - 1)
-    for copy in swaps():
-        copy.start()
+    for shift in range(1, SQUARE):
+        for copy in swaps(shift, False):
+            copy.start()
+    for stage in range(1, last):
+        for g in outer:
+            reduce(stage, g)
     for name in ("skip", "atom_cond", "atom_bias"):
         loads[name].wait()
     for halo in halos:
         halo.finish()
-    for copy in swaps():
-        copy.wait()
-    for stage in range(1, last):
-        for g in outer:
-            reduce(stage, g)
-        if stage == 1:
-            atom_before()
-    if last == 1:
-        atom_before()
+    for shift in range(1, SQUARE):
+        for copy in swaps(shift, False):
+            copy.wait_send()
+        for copy in swaps(shift, True):
+            copy.wait_recv()
+    atom_before()
     for side, present in ((0, me > 0), (1, me < last)):
 
         @pl.when(present)
         def _():
-            for part in (0, 1):
+            for part in range(PARTS):
                 take(side, me, part)
 
     token = (r.act[...].astype(jnp.float32) + r.total[me]).astype(jnp.bfloat16)
@@ -613,7 +628,7 @@
 
             @pl.when(goes)
             def _():
-                for part in (0, 1):
+                for part in range(PARTS):
                     hop(side, g, part).wait_send()
 
     rows_flow.finish()
@@ -636,6 +651,8 @@
     )
     packed = (groups, groups, rows // 2, 2 * width)
     chains = 4 + 2 * groups
+    high = atom_part.shape[0] // ATOM_MAPS
+    padded = high * SQUARE * -(-ATOM_MAPS // SQUARE)
     hops = max(groups - 1, 1)
     length = ring // 2
     scratch = {name: pltpu.VMEM(array.shape, array.dtype) for name, array in weights.items()}
@@ -655,7 +672,8 @@
         masked=pltpu.VMEM((count // WQ, HA * WQ, WK), jnp.float32),
         owner_rims=pltpu.VMEM((2, 1, near["owner"].shape[1]), jnp.int32),
         rows_all=pltpu.VMEM((ring, rows, channels), half_type),
-        atom_all=pltpu.VMEM((groups,) + atom_part.shape, half_type),
+        atom_pad=pltpu.VMEM((padded, channels), half_type),
+        atom_all=pltpu.VMEM((groups, padded, channels), half_type),
         conds=pltpu.VMEM((groups, rows, depth), half_type),
         act_out=pltpu.VMEM(packed[1:], half_type),
         acts=pltpu.VMEM(packed[1:], half_type),
@@ -683,10 +701,10 @@
         spread_recv=dma((2, ring)),
         halo_send=dma((3, 2)),
         halo_recv=dma((3, 2)),
-        swap_send=dma((2,)),
-        swap_recv=dma((2,)),
-        sum_send=dma((2, groups, 2)),
-        sum_recv=dma((2, groups, 2)),
+        swap_send=dma((2, SQUARE)),
+        swap_recv=dma((2, SQUARE)),
+        sum_send=dma((2, groups, PARTS)),
+        sum_recv=dma((2, groups, PARTS)),
     )
     names = ["bounds"] + list(near) + [name + "_hbm" for name in weights] + list(outs) + list(scratch)
     return pl.pallas_call(

time: 86 us -> 84.8 us (0.986)
  Pallas kernels: 85.2 us -> 84 us
    pallas_call x1, Pallas kernels: 83.6 us -> 82.3 us  [token_layer(): pl.pallas_call(functools.partial(token_kernel, tuple(names), groups, ring...]
where the time goes in v6:
time: 84.8 us; the launch traced here: 84.6 us
  Pallas kernels  84 us (99%)
    pallas_call x1, Pallas kernels, token_layer(): pl.pallas_call(functools.partial(token_kernel, tuple(names), groups, ring...  82.3 us

profile of v6, /device:TPU:0, one launch (start us, length us, event | category | flops | bytes accessed | tf_op | source)
XLA Modules:
  0.0 84.6 jit_solution(7748592973983646093)
XLA Ops:
  0.6 82.3 %token_layer.1 = (bf16[128,768]{1,0:T(8,128)(2,1)}, f32[3,1,1024]{2,1,0:T(1,128)}) custom-call(s32[2,32]{1,0:T(2,128)} %bitcast.22, bf16[128,768]{1,0:T(8,128)(2,1)} %bitcast.17, bf16[128,768]{1,0:T(8,128)(2,1)} %bitcast.18, s32[1,128]{1,0:T(1,128)} %bitcast.23, f32[3,768]{1,0:T(4,128)} %refs_4_.1, s32[8,128]{1,0:T(8,128)} %bitcast.20, ...), custom_call_target="tpu_custom_call" | custom-call | tf_op jit(solution)/shard_map/token_layer/pallas_call | solution.py:710
  83.0 1.6 %settle.1 = (bf16[128,768]{1,0:T(8,128)(2,1)}, f32[3,1,1024]{2,1,0:T(1,128)}) custom-call(bf16[128,768]{1,0:T(8,128)(2,1)} %get-tuple-element.6.token_ref, f32[3,1,1024]{2,1,0:T(1,128)} %get-tuple-element.7.update_ref), custom_call_target="tpu_custom_call" | custom-call | tf_op jit(solution)/shard_map/settle/pallas_call | solution.py:730

commit v7 on v6

--- a/solution.py
+++ b/solution.py
@@ -411,7 +411,7 @@
     for step in range(last - 1):
         for g in inner:
             attend_chains[g].arrive(step)
-    for g in outer:
+    for g in outer[:2]:
         transit_chains[g].begin()
     loads["attn"].wait()
     for g in inner:
@@ -457,20 +457,8 @@
         gate = jax.nn.sigmoid(r.gates[g].astype(jnp.float32))
         r.gated[g] = (result * gate).astype(jnp.bfloat16)
 
-    pending = [(transit_chains[g], step) for step in range(last - 1) for g in outer]
-    pending += [(flow, step) for step in range(last - 1) for flow in small_chains]
-    share = -(-len(pending) // groups)
     mask_flow.finish()
     loads["bias"].wait()
-    kv_flows[inner[0]].relay()
-    for number, g in enumerate(inner):
-        if number + 1 < groups:
-            kv_flows[inner[number + 1]].relay()
-        kv_flows[g].complete()
-        attention(g)
-        for flow, step in pending[number * share : (number + 1) * share]:
-            flow.arrive(step)
-
     def hop(side, g, part):
         piece = pl.ds(part * part_rows, part_rows)
         at = (side, g, part)
@@ -584,12 +572,35 @@
 
     for name in ("out", "tin", "tout"):
         loads[name].wait()
-    for g in outer:
-        transit_chains[g].arrive(last - 1)
+    def transition(g):
         full = joined(r.transit, g)
         hidden = jax.nn.silu(matmul(full, r.tin[0])) * matmul(full, r.tin[1])
         r.total[g] = matmul(r.gated[g], r.out[...]) + matmul(hidden.astype(jnp.bfloat16), r.tout[...])
         reduce(0, g)
+
+    def diagonal(number):
+        if 2 <= number + 1 < groups:
+            transit_chains[outer[number + 1]].begin()
+        for step in range(last):
+            if 0 <= number - step < groups:
+                transit_chains[outer[number - step]].arrive(step)
+                if step == last - 1:
+                    transition(outer[number - step])
+        if 0 <= number - last < last - 1:
+            for flow in small_chains:
+                flow.arrive(number - last)
+
+    kv_flows[inner[0]].relay()
+    diagonal(0)
+    for number, g in enumerate(inner):
+        if number + 1 < groups:
+            kv_flows[inner[number + 1]].relay()
+        kv_flows[g].complete()
+        attention(g)
+        if number + 1 != last - 1:
+            diagonal(number + 1 if number + 1 < last - 1 else number)
+    for number in range(groups, groups + last - 1):
+        diagonal(number)
     for flow in small_chains:
         flow.arrive(last - 1)
     for shift in range(1, SQUARE):

time: 84.8 us -> 80.9 us (0.954)
  Pallas kernels: 84 us -> 80.1 us
    pallas_call x1, Pallas kernels: 82.3 us -> 78.5 us  [token_layer(): pl.pallas_call(functools.partial(token_kernel, tuple(names), groups, ring...]
where the time goes in v7:
time: 80.9 us; the launch traced here: 80.7 us
  Pallas kernels  80.1 us (99%)
    pallas_call x1, Pallas kernels, token_layer(): pl.pallas_call(functools.partial(token_kernel, tuple(names), groups, ring...  78.5 us
    pallas_call x1, Pallas kernels, settle(): pl.pallas_call(settle_kernel, out_shape=tuple((jax.ShapeDtypeStruct(array...  1.62 us

profile of v7, /device:TPU:0, one launch (start us, length us, event | category | flops | bytes accessed | tf_op | source)
XLA Modules:
  0.0 80.7 jit_solution(10736410420684121311)
XLA Ops:
  0.6 78.5 %token_layer.1 = (bf16[128,768]{1,0:T(8,128)(2,1)}, f32[3,1,1024]{2,1,0:T(1,128)}) custom-call(s32[2,32]{1,0:T(2,128)} %bitcast.22, bf16[128,768]{1,0:T(8,128)(2,1)} %bitcast.17, bf16[128,768]{1,0:T(8,128)(2,1)} %bitcast.18, s32[1,128]{1,0:T(1,128)} %bitcast.23, f32[3,768]{1,0:T(4,128)} %refs_4_.1, s32[8,128]{1,0:T(8,128)} %bitcast.20, ...), custom_call_target="tpu_custom_call" | custom-call | tf_op jit(solution)/shard_map/token_layer/pallas_call | solution.py:721
  79.1 1.6 %settle.1 = (bf16[128,768]{1,0:T(8,128)(2,1)}, f32[3,1,1024]{2,1,0:T(1,128)}) custom-call(bf16[128,768]{1,0:T(8,128)(2,1)} %get-tuple-element.6.token_ref, f32[3,1,1024]{2,1,0:T(1,128)} %get-tuple-element.7.update_ref), custom_call_target="tpu_custom_call" | custom-call | tf_op jit(solution)/shard_map/settle/pallas_call | solution.py:741
